TPU v7x, 128 devices: a whole 4x4x4 slice. The times are simulated.
128 devices in a mesh: gx: 16 (over z, x), gy: 8 (over y, core).
Axes of the slice: x: 4, y: 4, z: 4, core: 2. Of those that a mesh axis runs over, the one named last changes fastest.
Arguments:
- pressure: float32 [10, 1024, 4096], P(None, 'gx', 'gy'), may hold values from -6 to 6
- pressure_old: float32 [10, 1024, 4096], P(None, 'gx', 'gy'), may hold values from -6 to 6
- conductivity: float32 [10, 1024, 4096], P(None, 'gx', 'gy'), may hold values from 0.1 to 1
- porosity: float32 [10, 1024, 4096], P(None, 'gx', 'gy'), may hold values from 2 to 8
- recharge: float32 [1024, 4096], P('gx', 'gy'), may hold values from -6 to 6
- active: int32 [1024, 4096], P('gx', 'gy'), may hold values from 0 to 1, as said below
Outputs:
- final_pressure: float32 [10, 1024, 4096], P(None, 'gx', 'gy')
- linear_residual: float32 [10, 1024, 4096], P(None, 'gx', 'gy')
Inputs may be any that keep to these rules, and one draw needn't show every extreme that they name: `active`: 1 marks a land column, 0 an ocean column.
All inputs are finite; a program needn't handle non-finite values.
Results may differ from a plain program's by a relative error of at most 0.0003.
Values sent between devices are 32-bit elements; how exact they have to be, the bound alone decides.
No kernel may reach another device: no remote copies, remote signals or barrier semaphores. Data moves between devices by JAX's collectives and lax.ppermute only.
A program may use at most 128 MiB of HBM per device.

v0:
```python
import jax
import jax.numpy as jnp
from jax import lax
from jax.sharding import Mesh
from jax.sharding import PartitionSpec as P

NEWTON = 2
GX_GY = ("gx_0", "gx_1", "gy_0", "gy_1")
GX = ("gx_0", "gx_1")
GY = ("gy_0", "gy_1")
residual_sat = 0.1
vertical_factor = 2.0
epsilon = 1e-06


def padded(value, sides, width):
    edges = {}
    for axis, dim in sides:
        size, length = (lax.axis_size(axis), value.shape[dim])
        up = [(i, (i + 1) % size) for i in range(size - 1)]
        last = lax.slice_in_dim(value, length - width, length, axis=dim)
        initial = lax.slice_in_dim(value, 0, width, axis=dim)
        edges[dim] = (
            lax.ppermute(last, axis, up),
            lax.ppermute(initial, axis, [(b, a) for a, b in up]),
        )
    done = []
    for _, dim in sides:
        low, high = edges[dim]
        around = [(width, width) if d in done else (0, 0) for d in range(value.ndim)]
        value = jnp.concatenate([jnp.pad(low, around), value, jnp.pad(high, around)], axis=dim)
        done.append(dim)
    return value


def by_axis(value, axes):
    for axis in axes:
        value = lax.psum(value, axis)
    return value


def interior(array):
    return array[:, 1:-1, 1:-1]


def saturation(values):
    return residual_sat + (1.0 - residual_sat) * jax.nn.sigmoid(values)


def sat_slope(values):
    sigma = jax.nn.sigmoid(values)
    return (1.0 - residual_sat) * sigma * (1.0 - sigma)


def face_pair(press_low, press_high, cond_low, cond_high, act_low, act_high, factor, gravity):
    transmit = 0.5 * factor * (cond_low + cond_high) * act_low * act_high
    sig_low = jax.nn.sigmoid(press_low)
    sig_high = jax.nn.sigmoid(press_high)
    mobility = 0.5 * (sig_low * sig_low + sig_high * sig_high)
    head_drop = press_low - press_high + gravity
    coef_low = transmit * (mobility + sig_low * sig_low * (1.0 - sig_low) * head_drop)
    coef_high = transmit * (sig_high * sig_high * (1.0 - sig_high) * head_drop - mobility)
    return (coef_low, coef_high, transmit * mobility * head_drop)


def coefficients(pressure, conduct, active):
    across_x = face_pair(
        pressure[:, :-1, 1:-1],
        pressure[:, 1:, 1:-1],
        conduct[:, :-1, 1:-1],
        conduct[:, 1:, 1:-1],
        active[:, :-1, 1:-1],
        active[:, 1:, 1:-1],
        1.0,
        0.0,
    )
    across_y = face_pair(
        pressure[:, 1:-1, :-1],
        pressure[:, 1:-1, 1:],
        conduct[:, 1:-1, :-1],
        conduct[:, 1:-1, 1:],
        active[:, 1:-1, :-1],
        active[:, 1:-1, 1:],
        1.0,
        0.0,
    )
    inner_p = interior(pressure)
    inner_k = interior(conduct)
    inner_a = interior(active)
    across_z = face_pair(
        inner_p[:-1],
        inner_p[1:],
        inner_k[:-1],
        inner_k[1:],
        inner_a[:-1],
        inner_a[1:],
        vertical_factor,
        -1.0,
    )
    return (across_x, across_y, across_z)


def outflow(flow_x, flow_y, flow_z):
    total = flow_x[:, 1:] - flow_x[:, :-1] + flow_y[:, :, 1:] - flow_y[:, :, :-1]
    zeros = jnp.zeros_like(flow_z[:1])
    return total + jnp.concatenate([flow_z, zeros], 0) - jnp.concatenate([zeros, flow_z], 0)


def jacobian_apply(vector, faces, diagonal, active):
    x_low, x_high, x_flow = faces[0]
    y_low, y_high, y_flow = faces[1]
    z_low, z_high, z_flow = faces[2]
    flow_x = x_low * vector[:, :-1, 1:-1] + x_high * vector[:, 1:, 1:-1]
    flow_y = y_low * vector[:, 1:-1, :-1] + y_high * vector[:, 1:-1, 1:]
    center = interior(vector)
    flow_z = z_low * center[:-1] + z_high * center[1:]
    return active * (diagonal * center + outflow(flow_x, flow_y, flow_z)) + (1.0 - active) * center


def newton_residual(pressure, faces, pressure_old, porosity, recharge, active):
    center = interior(pressure)
    storage = porosity * (saturation(center) - saturation(pressure_old))
    inflow = jnp.concatenate([jnp.zeros_like(center[:-1]), recharge[None]], 0)
    flows = outflow(faces[0][2], faces[1][2], faces[2][2])
    return active * (storage - inflow + flows) + (1.0 - active) * center


def least_squares(first_norm, entry_one, entry_two, entry_three, entry_four, entry_five):
    radius = jnp.sqrt(entry_one * entry_one + entry_two * entry_two)
    cosine = entry_one / radius
    sine = entry_two / radius
    top_right = cosine * entry_three + sine * entry_four
    lower = cosine * entry_four - sine * entry_three
    weight_two = -lower * sine * first_norm / (lower * lower + entry_five * entry_five)
    weight_one = (cosine * first_norm - top_right * weight_two) / radius
    return (weight_one, weight_two)


def body(pressure, pressure_old, conductivity, porosity, recharge, active):
    layers = pressure.shape[0]
    active_flat = active.astype(jnp.float32)
    active_cells = jnp.broadcast_to(active_flat[None], pressure.shape)
    stacked = jnp.concatenate([conductivity, active_flat[None]], 0)
    widened = padded(stacked, ((GX, 1), (GY, 2)), 1)
    cond_ext = widened[:layers]
    act_ext = jnp.broadcast_to(widened[layers][None], cond_ext.shape)
    current = pressure
    leftover = jnp.zeros_like(pressure)
    for newton_index in range(NEWTON):
        diagonal = porosity * sat_slope(current)
        current_ext = padded(current, ((GX, 1), (GY, 2)), 1)
        faces = coefficients(current_ext, cond_ext, act_ext)
        remainder = -newton_residual(
            current_ext, faces, pressure_old, porosity, recharge, active_cells
        )
        first_norm = jnp.sqrt(by_axis(jnp.sum(remainder * remainder), GX_GY) + epsilon)
        basis_one = remainder / first_norm
        basis_ext = padded(basis_one, ((GX, 1), (GY, 2)), 1)
        image_one = jacobian_apply(basis_ext, faces, diagonal, active_cells)
        entry_one, square_one = (
            by_axis(jnp.sum(image_one * basis_one), GX_GY),
            by_axis(jnp.sum(image_one * image_one), GX_GY),
        )
        ortho_one = image_one - entry_one * basis_one
        entry_two = jnp.sqrt(square_one - entry_one * entry_one + epsilon)
        basis_two = ortho_one / entry_two
        second_ext = padded(basis_two, ((GX, 1), (GY, 2)), 1)
        image_two = jacobian_apply(second_ext, faces, diagonal, active_cells)
        entry_three, entry_four, square_two = (
            by_axis(jnp.sum(image_two * basis_one), GX_GY),
            by_axis(jnp.sum(image_two * basis_two), GX_GY),
            by_axis(jnp.sum(image_two * image_two), GX_GY),
        )
        entry_five = jnp.sqrt(
            square_two - entry_three * entry_three - entry_four * entry_four + epsilon
        )
        weight_one, weight_two = least_squares(
            first_norm, entry_one, entry_two, entry_three, entry_four, entry_five
        )
        current = current + (weight_one * basis_one + weight_two * basis_two)
        leftover = remainder - weight_one * image_one - weight_two * image_two
    return (current, leftover)


def solution(mesh):
    torus = Mesh(mesh.devices.reshape(4, 4, 4, 2), ("gx_0", "gx_1", "gy_0", "gy_1"))
    in_specs = (
        P(None, GX, GY),
        P(None, GX, GY),
        P(None, GX, GY),
        P(None, GX, GY),
        P(GX, GY),
        P(GX, GY),
    )
    out_specs = (P(None, GX, GY), P(None, GX, GY))
    return jax.shard_map(body, mesh=torus, in_specs=in_specs, out_specs=out_specs, check_vma=False)
```

profile of v0, /device:TPU:1, one launch (start us, length us, event | category | flops | bytes accessed | tf_op | source)
XLA Modules:
  0.0 389.7 jit_solution(7502140902498342127)
XLA Ops:
  3.4 3.9 %collective-permute-start = (f32[11,1,512]{2,1,0:T(1,128)}, f32[11,1,512]{2,1,0:T(1,128)S(1)}, u32[]{:S(2)}, u32[]{:S(2)}) collective-permute-start(f32[11,1,512]{2,1,0:T(1,128)} %get-tuple-element.72), channel_id=1, source_target_pairs={{0,8},{8,16},{16,24},{24,32},{32,40},{40,48},{48,56},{56,64},{64,7... | collective-permute-start | bytes 67592 | tf_op jit(solution)/shard_map/ppermute | solution.py:24
  9.0 4.0 %collective-permute-start.2 = (f32[11,64,1]{2,1,0:T(8,128)S(1)}, f32[11,64,1]{2,1,0:T(8,128)S(1)}, u32[]{:S(2)}, u32[]{:S(2)}) collective-permute-start(f32[11,64,1]{2,1,0:T(8,128)S(1)} %get-tuple-element.74), channel_id=1, source_target_pairs={{0,1},{1,2},{2,3},{3,4},{4,5},{5,6},{6,7},{8,9},{9,10},{10,11},{11... | collective-permute-start | bytes 8456 | tf_op jit(solution)/shard_map/ppermute | solution.py:24
  13.1 1.9 collective-permute-start.3
  18.5 4.9 %collective-permute-start.4 = (f32[10,1,512]{2,1,0:T(1,128)S(1)}, f32[10,1,512]{2,1,0:T(1,128)S(1)}, u32[]{:S(2)}, u32[]{:S(2)}) collective-permute-start(f32[10,1,512]{2,1,0:T(1,128)S(1)} %get-tuple-element.98), channel_id=1, source_target_pairs={{0,8},{8,16},{16,24},{24,32},{32,40},{40,48},{48,56},{56,64},{64,7... | collective-permute-start | bytes 61448 | tf_op jit(solution)/shard_map/ppermute | solution.py:24
  23.4 3.9 %collective-permute-start.6 = (f32[10,64,1]{2,1,0:T(8,128)}, f32[10,64,1]{2,1,0:T(8,128)}, u32[]{:S(2)}, u32[]{:S(2)}) collective-permute-start(f32[10,64,1]{2,1,0:T(8,128)} %get-tuple-element.96), channel_id=1, source_target_pairs={{0,1},{1,2},{2,3},{3,4},{4,5},{5,6},{6,7},{8,9},{9,10},{10,11},{11... | collective-permute-start | bytes 7688 | tf_op jit(solution)/shard_map/ppermute | solution.py:24
  36.9 5.1 %multiply_multiply_fusion.1 = (f32[10,64,513]{2,1,0:T(8,128)S(1)}, f32[10,64,513]{2,1,0:T(8,128)}) fusion(f32[10,64,1]{2,1,0:T(8,128)} %collective-permute-done.7, f32[10,1,512]{2,1,0:T(1,128)S(1)} %collective-permute-done.5, f32[10,64,512]{2,1,0:T(8,128)S(1)} %copy-done, f32[10,1,512]{2,1,0:T(1,128)S(1)} %collective-permute-done.4, ...), kind=kLoop, calls=%fused_computation.83 | loop fusion | flops 11162880 | bytes 5738672 | tf_op jit(solution)/shard_map/mul | solution.py:63
  42.1 2.9 multiply_reduce_fusion.11
  45.0 13.0 %psum.336 = f32[]{:T(128)} all-reduce(f32[]{:T(128)} %get-tuple-element.66), channel_id=1, replica_groups=mesh['gx_0'=4,'gx_1'=4,'gy_0'=4,'gy_1'=2] {'gx_0'}, use_global_device_ids=true, to_apply=%region_1.2 | all-reduce | flops 1 | bytes 8 | tf_op jit(solution)/shard_map/psum | solution.py:38
  57.9 7.2 %psum.337 = f32[]{:T(128)} all-reduce(f32[]{:T(128)} %psum.336), channel_id=1, replica_groups=mesh['gx_0'=4,'gx_1'=4,'gy_0'=4,'gy_1'=2] {'gx_1'}, use_global_device_ids=true, to_apply=%region_2.3 | all-reduce | flops 1 | bytes 8 | tf_op jit(solution)/shard_map/psum | solution.py:38
  65.1 8.0 %psum.338 = f32[]{:T(128)} all-reduce(f32[]{:T(128)} %psum.337), channel_id=1, replica_groups=mesh['gx_0'=4,'gx_1'=4,'gy_0'=4,'gy_1'=2] {'gy_0'}, use_global_device_ids=true, to_apply=%region_3.4 | all-reduce | flops 1 | bytes 8 | tf_op jit(solution)/shard_map/psum | solution.py:38
  73.1 9.5 %psum.339 = f32[]{:T(128)} all-reduce(f32[]{:T(128)} %psum.338), channel_id=1, replica_groups=mesh['gx_0'=4,'gx_1'=4,'gy_0'=4,'gy_1'=2] {'gy_1'}, use_global_device_ids=true, to_apply=%region_4.5 | all-reduce | flops 1 | bytes 8 | tf_op jit(solution)/shard_map/psum | solution.py:38
  85.1 3.0 collective-permute-start.8
  89.4 1.9 collective-permute-start.10
  91.3 2.4 collective-permute-start.11
  95.1 3.1 fusion.30
  99.7 4.4 %fusion.19 = (f32[10,64,513]{2,1,0:T(8,128)S(1)}, f32[10,64,513]{2,1,0:T(8,128)}, f32[10,64,513]{2,1,0:T(8,128)}) fusion(f32[10,64,1]{2,1,0:T(8,128)S(1)} %collective-permute-done.11, f32[10,1,512]{2,1,0:T(1,128)S(1)} %collective-permute-done.9, f32[10,64,512]{2,1,0:T(8,128)S(1)} %negate_divide_fusion, f32[10,1,512]{2,1,0:T(1,128)S(1)} %collective-permute-done.8, ...), kind=kLoop, calls=%fused_computation.46 | loop fusion | flops 13789440 | bytes 7966720 | tf_op jit(solution)/shard_map/add | solution.py:114
  104.2 3.0 multiply_reduce_fusion.10
  107.1 10.9 %all-reduce.38 = (f32[]{:T(128)}, f32[]{:T(128)}) all-reduce(f32[]{:T(128)} %get-tuple-element.11, f32[]{:T(128)} %get-tuple-element.10), channel_id=1, replica_groups=mesh['gx_0'=4,'gx_1'=4,'gy_0'=4,'gy_1'=2] {'gx_0'}, use_global_device_ids=true, to_apply=%region_11.12 | all-reduce | flops 2 | bytes 16 | tf_op jit(solution)/shard_map/psum | solution.py:38
  118.1 6.7 %all-reduce.34 = (f32[]{:T(128)}, f32[]{:T(128)}) all-reduce(f32[]{:T(128)} %get-tuple-element.40, f32[]{:T(128)} %get-tuple-element.41), channel_id=1, replica_groups=mesh['gx_0'=4,'gx_1'=4,'gy_0'=4,'gy_1'=2] {'gx_1'}, use_global_device_ids=true, to_apply=%region_12.13 | all-reduce | flops 2 | bytes 16 | tf_op jit(solution)/shard_map/psum | solution.py:38
  124.8 7.6 %all-reduce.30 = (f32[]{:T(128)}, f32[]{:T(128)}) all-reduce(f32[]{:T(128)} %get-tuple-element.30, f32[]{:T(128)} %get-tuple-element.31), channel_id=1, replica_groups=mesh['gx_0'=4,'gx_1'=4,'gy_0'=4,'gy_1'=2] {'gy_0'}, use_global_device_ids=true, to_apply=%region_13.14 | all-reduce | flops 2 | bytes 16 | tf_op jit(solution)/shard_map/psum | solution.py:38
  132.4 7.7 %all-reduce.42 = (f32[]{:T(128)}, f32[]{:T(128)}) all-reduce(f32[]{:T(128)} %get-tuple-element.20, f32[]{:T(128)} %get-tuple-element.21), channel_id=1, replica_groups=mesh['gx_0'=4,'gx_1'=4,'gy_0'=4,'gy_1'=2] {'gy_1'}, use_global_device_ids=true, to_apply=%region_14.15 | all-reduce | flops 2 | bytes 16 | tf_op jit(solution)/shard_map/psum | solution.py:38
  141.9 2.8 subtract_divide_fusion.1
  146.6 3.6 collective-permute-start.12
  153.1 2.6 collective-permute-start.14
  155.7 2.5 collective-permute-start.15
  158.2 2.5 fusion.31
  160.8 3.7 collective-permute-done.15
  166.7 2.0 multiply_reduce_fusion.6
  168.7 10.3 %all-reduce.37 = (f32[]{:T(128)}, f32[]{:T(128)}, f32[]{:T(128)}) all-reduce(f32[]{:T(128)} %get-tuple-element.8, f32[]{:T(128)} %get-tuple-element.9, f32[]{:T(128)} %get-tuple-element.7), channel_id=1, replica_groups=mesh['gx_0'=4,'gx_1'=4,'gy_0'=4,'gy_1'=2] {'gx_0'}, use_global_device_ids=true, to_apply=%region_21.22 | all-reduce | flops 3 | bytes 24 | tf_op jit(solution)/shard_map/psum | solution.py:38
  179.0 6.7 %all-reduce.33 = (f32[]{:T(128)}, f32[]{:T(128)}, f32[]{:T(128)}) all-reduce(f32[]{:T(128)} %get-tuple-element.37, f32[]{:T(128)} %get-tuple-element.38, f32[]{:T(128)} %get-tuple-element.39), channel_id=1, replica_groups=mesh['gx_0'=4,'gx_1'=4,'gy_0'=4,'gy_1'=2] {'gx_1'}, use_global_device_ids=true, to_apply=%region_22.23 | all-reduce | flops 3 | bytes 24 | tf_op jit(solution)/shard_map/psum | solution.py:38
  185.7 6.7 %all-reduce.29 = (f32[]{:T(128)}, f32[]{:T(128)}, f32[]{:T(128)}) all-reduce(f32[]{:T(128)} %get-tuple-element.27, f32[]{:T(128)} %get-tuple-element.28, f32[]{:T(128)} %get-tuple-element.29), channel_id=1, replica_groups=mesh['gx_0'=4,'gx_1'=4,'gy_0'=4,'gy_1'=2] {'gy_0'}, use_global_device_ids=true, to_apply=%region_23.24 | all-reduce | flops 3 | bytes 24 | tf_op jit(solution)/shard_map/psum | solution.py:38
  192.4 8.5 %all-reduce.41 = (f32[]{:T(128)}, f32[]{:T(128)}, f32[]{:T(128)}) all-reduce(f32[]{:T(128)} %get-tuple-element.17, f32[]{:T(128)} %get-tuple-element.18, f32[]{:T(128)} %get-tuple-element.19), channel_id=1, replica_groups=mesh['gx_0'=4,'gx_1'=4,'gy_0'=4,'gy_1'=2] {'gy_1'}, use_global_device_ids=true, to_apply=%region_24.25 | all-reduce | flops 3 | bytes 24 | tf_op jit(solution)/shard_map/psum | solution.py:38
  207.0 2.3 add_add_fusion.1
  209.8 3.8 collective-permute-start.16
  215.1 1.9 collective-permute-start.18
  217.0 2.6 collective-permute-start.19
  221.0 4.5 %collective-permute-done.19 = f32[10,64,1]{2,1,0:T(8,128)S(1)} collective-permute-done((f32[10,64,1]{2,1,0:T(8,128)S(1)}, f32[10,64,1]{2,1,0:T(8,128)S(1)}, u32[]{:S(2)}, u32[]{:S(2)}) %collective-permute-start.19) | collective-permute-done | bytes 2592 | tf_op jit(solution)/shard_map/ppermute | solution.py:25
  226.9 2.9 multiply_reduce_fusion.5
  229.7 9.8 %psum.360 = f32[]{:T(128)} all-reduce(f32[]{:T(128)} %get-tuple-element.57), channel_id=1, replica_groups=mesh['gx_0'=4,'gx_1'=4,'gy_0'=4,'gy_1'=2] {'gx_0'}, use_global_device_ids=true, to_apply=%region_31.32 | all-reduce | flops 1 | bytes 8 | tf_op jit(solution)/shard_map/psum | solution.py:38
  239.5 6.7 %psum.361 = f32[]{:T(128)} all-reduce(f32[]{:T(128)} %psum.360), channel_id=1, replica_groups=mesh['gx_0'=4,'gx_1'=4,'gy_0'=4,'gy_1'=2] {'gx_1'}, use_global_device_ids=true, to_apply=%region_32.33 | all-reduce | flops 1 | bytes 8 | tf_op jit(solution)/shard_map/psum | solution.py:38
  246.2 7.4 %psum.362 = f32[]{:T(128)} all-reduce(f32[]{:T(128)} %psum.361), channel_id=1, replica_groups=mesh['gx_0'=4,'gx_1'=4,'gy_0'=4,'gy_1'=2] {'gy_0'}, use_global_device_ids=true, to_apply=%region_33.34 | all-reduce | flops 1 | bytes 8 | tf_op jit(solution)/shard_map/psum | solution.py:38
  253.6 7.7 %psum.363 = f32[]{:T(128)} all-reduce(f32[]{:T(128)} %psum.362), channel_id=1, replica_groups=mesh['gx_0'=4,'gx_1'=4,'gy_0'=4,'gy_1'=2] {'gy_1'}, use_global_device_ids=true, to_apply=%region_34.35 | all-reduce | flops 1 | bytes 8 | tf_op jit(solution)/shard_map/psum | solution.py:38
  264.5 3.6 collective-permute-start.20
  269.6 2.6 collective-permute-start.22
  272.3 2.3 collective-permute-start.23
  276.4 4.4 %collective-permute-done.23 = f32[10,64,1]{2,1,0:T(8,128)S(1)} collective-permute-done((f32[10,64,1]{2,1,0:T(8,128)S(1)}, f32[10,64,1]{2,1,0:T(8,128)S(1)}, u32[]{:S(2)}, u32[]{:S(2)}) %collective-permute-start.23) | collective-permute-done | bytes 2592 | tf_op jit(solution)/shard_map/ppermute | solution.py:25
  280.8 3.3 fusion.7
  284.1 2.9 multiply_reduce_fusion.4
  287.1 10.3 %all-reduce.36 = (f32[]{:T(128)}, f32[]{:T(128)}) all-reduce(f32[]{:T(128)} %get-tuple-element.6, f32[]{:T(128)} %get-tuple-element.5), channel_id=1, replica_groups=mesh['gx_0'=4,'gx_1'=4,'gy_0'=4,'gy_1'=2] {'gx_0'}, use_global_device_ids=true, to_apply=%region_41.42 | all-reduce | flops 2 | bytes 16 | tf_op jit(solution)/shard_map/psum | solution.py:38
  297.4 6.7 %all-reduce.32 = (f32[]{:T(128)}, f32[]{:T(128)}) all-reduce(f32[]{:T(128)} %get-tuple-element.35, f32[]{:T(128)} %get-tuple-element.36), channel_id=1, replica_groups=mesh['gx_0'=4,'gx_1'=4,'gy_0'=4,'gy_1'=2] {'gx_1'}, use_global_device_ids=true, to_apply=%region_42.43 | all-reduce | flops 2 | bytes 16 | tf_op jit(solution)/shard_map/psum | solution.py:38
  304.1 6.7 %all-reduce.28 = (f32[]{:T(128)}, f32[]{:T(128)}) all-reduce(f32[]{:T(128)} %get-tuple-element.25, f32[]{:T(128)} %get-tuple-element.26), channel_id=1, replica_groups=mesh['gx_0'=4,'gx_1'=4,'gy_0'=4,'gy_1'=2] {'gy_0'}, use_global_device_ids=true, to_apply=%region_43.44 | all-reduce | flops 2 | bytes 16 | tf_op jit(solution)/shard_map/psum | solution.py:38
  310.8 8.5 %all-reduce.40 = (f32[]{:T(128)}, f32[]{:T(128)}) all-reduce(f32[]{:T(128)} %get-tuple-element.15, f32[]{:T(128)} %get-tuple-element.16), channel_id=1, replica_groups=mesh['gx_0'=4,'gx_1'=4,'gy_0'=4,'gy_1'=2] {'gy_1'}, use_global_device_ids=true, to_apply=%region_44.45 | all-reduce | flops 2 | bytes 16 | tf_op jit(solution)/shard_map/psum | solution.py:38
  321.3 2.7 subtract_divide_fusion
  325.9 3.6 collective-permute-start.24
  332.6 1.9 collective-permute-start.26
  334.5 3.1 collective-permute-start.27
  337.7 3.3 fusion.33
  341.0 2.2 collective-permute-done.27
  345.5 2.9 multiply_reduce_fusion
  348.4 9.8 %all-reduce.35 = (f32[]{:T(128)}, f32[]{:T(128)}, f32[]{:T(128)}) all-reduce(f32[]{:T(128)} %get-tuple-element.3, f32[]{:T(128)} %get-tuple-element.4, f32[]{:T(128)} %get-tuple-element.2), channel_id=1, replica_groups=mesh['gx_0'=4,'gx_1'=4,'gy_0'=4,'gy_1'=2] {'gx_0'}, use_global_device_ids=true, to_apply=%region_51.52 | all-reduce | flops 3 | bytes 24 | tf_op jit(solution)/shard_map/psum | solution.py:38
  358.3 6.6 %all-reduce.31 = (f32[]{:T(128)}, f32[]{:T(128)}, f32[]{:T(128)}) all-reduce(f32[]{:T(128)} %get-tuple-element.32, f32[]{:T(128)} %get-tuple-element.33, f32[]{:T(128)} %get-tuple-element.34), channel_id=1, replica_groups=mesh['gx_0'=4,'gx_1'=4,'gy_0'=4,'gy_1'=2] {'gx_1'}, use_global_device_ids=true, to_apply=%region_52.53 | all-reduce | flops 3 | bytes 24 | tf_op jit(solution)/shard_map/psum | solution.py:38
  364.9 7.5 %all-reduce.27 = (f32[]{:T(128)}, f32[]{:T(128)}, f32[]{:T(128)}) all-reduce(f32[]{:T(128)} %get-tuple-element.22, f32[]{:T(128)} %get-tuple-element.23, f32[]{:T(128)} %get-tuple-element.24), channel_id=1, replica_groups=mesh['gx_0'=4,'gx_1'=4,'gy_0'=4,'gy_1'=2] {'gy_0'}, use_global_device_ids=true, to_apply=%region_53.54 | all-reduce | flops 3 | bytes 24 | tf_op jit(solution)/shard_map/psum | solution.py:38
  372.4 7.7 %all-reduce.39 = (f32[]{:T(128)}, f32[]{:T(128)}, f32[]{:T(128)}) all-reduce(f32[]{:T(128)} %get-tuple-element.12, f32[]{:T(128)} %get-tuple-element.13, f32[]{:T(128)} %get-tuple-element.14), channel_id=1, replica_groups=mesh['gx_0'=4,'gx_1'=4,'gy_0'=4,'gy_1'=2] {'gy_1'}, use_global_device_ids=true, to_apply=%region_54.55 | all-reduce | flops 3 | bytes 24 | tf_op jit(solution)/shard_map/psum | solution.py:38
  385.3 4.4 %multiply_subtract_fusion = (f32[10,64,512]{2,1,0:T(8,128)}, f32[10,64,512]{2,1,0:T(8,128)}) fusion(f32[10,64,512]{2,1,0:T(8,128)} %get-tuple-element.52, f32[10,64,512]{2,1,0:T(8,128)} %get-tuple-element.53, f32[10,64,512]{2,1,0:T(8,128)} %get-tuple-element.58, f32[]{:T(128)S(6)} %div.125, f32[]{:T(128)S(6)} %div.126, ...), kind=kLoop, calls=%fused_computation.169 | loop fusion | flops 3276800 | bytes 9175052 | tf_op jit(solution)/shard_map/sub | solution.py:181
  (160 shorter events, 46.4 us)
Async XLA Ops:
  0.6 8.2 %copy-start.1 = (f32[10,64,512]{2,1,0:T(8,128)S(1)}, f32[10,64,512]{2,1,0:T(8,128)}, u32[]{:S(2)}) copy-start(f32[10,64,512]{2,1,0:T(8,128)} %param.8) | copy-start | bytes 3932164
  1.7 13.3 %copy-start = (f32[10,64,512]{2,1,0:T(8,128)S(1)}, f32[10,64,512]{2,1,0:T(8,128)}, u32[]{:S(2)}) copy-start(f32[10,64,512]{2,1,0:T(8,128)} %param.6) | copy-start | bytes 3932164
  3.4 28.3 %collective-permute-start = (f32[11,1,512]{2,1,0:T(1,128)}, f32[11,1,512]{2,1,0:T(1,128)S(1)}, u32[]{:S(2)}, u32[]{:S(2)}) collective-permute-start(f32[11,1,512]{2,1,0:T(1,128)} %get-tuple-element.72), channel_id=1, source_target_pairs={{0,8},{8,16},{16,24},{24,32},{32,40},{40,48},{48,56},{56,64},{64,7... | collective-permute-start | bytes 67592 | tf_op jit(solution)/shard_map/ppermute | solution.py:24
  7.4 9.9 %copy-start.44 = (s32[64,512]{1,0:T(8,128)S(1)}, s32[64,512]{1,0:T(8,128)}, u32[]{:S(2)}) copy-start(s32[64,512]{1,0:T(8,128)} %param.11) | copy-start | bytes 393220
  7.4 24.4 %collective-permute-start.1 = (f32[11,1,512]{2,1,0:T(1,128)S(1)}, f32[11,1,512]{2,1,0:T(1,128)S(1)}, u32[]{:S(2)}, u32[]{:S(2)}) collective-permute-start(f32[11,1,512]{2,1,0:T(1,128)S(1)} %get-tuple-element.73), channel_id=1, source_target_pairs={{8,0},{16,8},{24,16},{32,24},{40,32},{48,40},{56,48},{64,56},{72,6... | collective-permute-start | bytes 67592 | tf_op jit(solution)/shard_map/ppermute | solution.py:25
  9.0 9.5 %collective-permute-start.2 = (f32[11,64,1]{2,1,0:T(8,128)S(1)}, f32[11,64,1]{2,1,0:T(8,128)S(1)}, u32[]{:S(2)}, u32[]{:S(2)}) collective-permute-start(f32[11,64,1]{2,1,0:T(8,128)S(1)} %get-tuple-element.74), channel_id=1, source_target_pairs={{0,1},{1,2},{2,3},{3,4},{4,5},{5,6},{6,7},{8,9},{9,10},{10,11},{11... | collective-permute-start | bytes 8456 | tf_op jit(solution)/shard_map/ppermute | solution.py:24
  13.1 10.4 %collective-permute-start.3 = (f32[11,64,1]{2,1,0:T(8,128)S(1)}, f32[11,64,1]{2,1,0:T(8,128)S(1)}, u32[]{:S(2)}, u32[]{:S(2)}) collective-permute-start(f32[11,64,1]{2,1,0:T(8,128)S(1)} %get-tuple-element.75), channel_id=1, source_target_pairs={{1,0},{2,1},{3,2},{4,3},{5,4},{6,5},{7,6},{9,8},{10,9},{11,10},{12... | collective-permute-start | bytes 8456 | tf_op jit(solution)/shard_map/ppermute | solution.py:25
  15.0 13.1 %collective-permute-start.5 = (f32[10,1,512]{2,1,0:T(1,128)S(1)}, f32[10,1,512]{2,1,0:T(1,128)S(1)}, u32[]{:S(2)}, u32[]{:S(2)}) collective-permute-start(f32[10,1,512]{2,1,0:T(1,128)S(1)} %get-tuple-element.99), channel_id=1, source_target_pairs={{8,0},{16,8},{24,16},{32,24},{40,32},{48,40},{56,48},{64,56},{72,6... | collective-permute-start | bytes 61448 | tf_op jit(solution)/shard_map/ppermute | solution.py:25
  18.5 16.1 %collective-permute-start.4 = (f32[10,1,512]{2,1,0:T(1,128)S(1)}, f32[10,1,512]{2,1,0:T(1,128)S(1)}, u32[]{:S(2)}, u32[]{:S(2)}) collective-permute-start(f32[10,1,512]{2,1,0:T(1,128)S(1)} %get-tuple-element.98), channel_id=1, source_target_pairs={{0,8},{8,16},{16,24},{24,32},{32,40},{40,48},{48,56},{56,64},{64,7... | collective-permute-start | bytes 61448 | tf_op jit(solution)/shard_map/ppermute | solution.py:24
  23.4 9.2 %copy-start.35 = (f32[11,66,1]{2,1,0:T(8,128)}, f32[11,66,1]{2,1,0:T(8,128)S(1)}, u32[]{:S(2)}) copy-start(f32[11,66,1]{2,1,0:T(8,128)S(1)} %pad.57) | copy-start | bytes 8716
  23.4 12.4 %collective-permute-start.6 = (f32[10,64,1]{2,1,0:T(8,128)}, f32[10,64,1]{2,1,0:T(8,128)}, u32[]{:S(2)}, u32[]{:S(2)}) collective-permute-start(f32[10,64,1]{2,1,0:T(8,128)} %get-tuple-element.96), channel_id=1, source_target_pairs={{0,1},{1,2},{2,3},{3,4},{4,5},{5,6},{6,7},{8,9},{9,10},{10,11},{11... | collective-permute-start | bytes 7688 | tf_op jit(solution)/shard_map/ppermute | solution.py:24
  28.2 8.7 %collective-permute-start.7 = (f32[10,64,1]{2,1,0:T(8,128)}, f32[10,64,1]{2,1,0:T(8,128)}, u32[]{:S(2)}, u32[]{:S(2)}) collective-permute-start(f32[10,64,1]{2,1,0:T(8,128)} %get-tuple-element.97), channel_id=1, source_target_pairs={{1,0},{2,1},{3,2},{4,3},{5,4},{6,5},{7,6},{9,8},{10,9},{11,10},{12... | collective-permute-start | bytes 7688 | tf_op jit(solution)/shard_map/ppermute | solution.py:25
  34.6 2.3 copy-start.36
  34.6 2.3 copy-start.37
  36.9 5.2 %copy-start.7 = (f32[10,64,512]{2,1,0:T(8,128)S(1)}, f32[10,64,512]{2,1,0:T(8,128)}, u32[]{:S(2)}) copy-start(f32[10,64,512]{2,1,0:T(8,128)} %param.9) | copy-start | bytes 3932164
  36.9 5.2 %copy-start.31 = (f32[10,64,512]{2,1,0:T(8,128)S(1)}, f32[10,64,512]{2,1,0:T(8,128)}, u32[]{:S(2)}) copy-start(f32[10,64,512]{2,1,0:T(8,128)} %param.7) | copy-start | bytes 3932164
  36.9 5.2 %copy-start.42 = (f32[64,512]{1,0:T(8,128)S(1)}, f32[64,512]{1,0:T(8,128)}, u32[]{:S(2)}) copy-start(f32[64,512]{1,0:T(8,128)} %param.10) | copy-start | bytes 393220
  83.3 10.5 %copy-start.17 = (f32[9,64,512]{2,1,0:T(8,128)S(1)}, f32[9,64,512]{2,1,0:T(8,128)}, u32[]{:S(2)}) copy-start(f32[9,64,512]{2,1,0:T(8,128)} %get-tuple-element.69) | copy-start | bytes 3538948
  85.1 9.5 %collective-permute-start.8 = (f32[10,1,512]{2,1,0:T(1,128)S(1)}, f32[10,1,512]{2,1,0:T(1,128)S(1)}, u32[]{:S(2)}, u32[]{:S(2)}) collective-permute-start(f32[10,1,512]{2,1,0:T(1,128)S(1)} %get-tuple-element.94), channel_id=1, source_target_pairs={{0,8},{8,16},{16,24},{24,32},{32,40},{40,48},{48,56},{56,64},{64,7... | collective-permute-start | bytes 61448 | tf_op jit(solution)/shard_map/ppermute | solution.py:24
  88.1 6.5 %collective-permute-start.9 = (f32[10,1,512]{2,1,0:T(1,128)S(1)}, f32[10,1,512]{2,1,0:T(1,128)S(1)}, u32[]{:S(2)}, u32[]{:S(2)}) collective-permute-start(f32[10,1,512]{2,1,0:T(1,128)S(1)} %get-tuple-element.95), channel_id=1, source_target_pairs={{8,0},{16,8},{24,16},{32,24},{40,32},{48,40},{56,48},{64,56},{72,6... | collective-permute-start | bytes 61448 | tf_op jit(solution)/shard_map/ppermute | solution.py:25
  89.4 8.8 %collective-permute-start.10 = (f32[10,64,1]{2,1,0:T(8,128)S(1)}, f32[10,64,1]{2,1,0:T(8,128)S(1)}, u32[]{:S(2)}, u32[]{:S(2)}) collective-permute-start(f32[10,64,1]{2,1,0:T(8,128)S(1)} %get-tuple-element.92), channel_id=1, source_target_pairs={{0,1},{1,2},{2,3},{3,4},{4,5},{5,6},{6,7},{8,9},{9,10},{10,11},{11... | collective-permute-start | bytes 7688 | tf_op jit(solution)/shard_map/ppermute | solution.py:24
  91.3 8.4 %collective-permute-start.11 = (f32[10,64,1]{2,1,0:T(8,128)S(1)}, f32[10,64,1]{2,1,0:T(8,128)S(1)}, u32[]{:S(2)}, u32[]{:S(2)}) collective-permute-start(f32[10,64,1]{2,1,0:T(8,128)S(1)} %get-tuple-element.93), channel_id=1, source_target_pairs={{1,0},{2,1},{3,2},{4,3},{5,4},{6,5},{7,6},{9,8},{10,9},{11,10},{12... | collective-permute-start | bytes 7688 | tf_op jit(solution)/shard_map/ppermute | solution.py:25
  94.6 5.1 %copy-start.22 = (f32[10,64,513]{2,1,0:T(8,128)S(1)}, f32[10,64,513]{2,1,0:T(8,128)}, u32[]{:S(2)}) copy-start(f32[10,64,513]{2,1,0:T(8,128)} %get-tuple-element.71) | copy-start | bytes 3939844
  99.7 4.5 %copy-start.8 = (f32[10,64,512]{2,1,0:T(8,128)S(1)}, f32[10,64,512]{2,1,0:T(8,128)}, u32[]{:S(2)}) copy-start(f32[10,64,512]{2,1,0:T(8,128)} %param.9) | copy-start | bytes 3932164
  99.7 4.5 %copy-start.13 = (f32[10,64,512]{2,1,0:T(8,128)S(1)}, f32[10,64,512]{2,1,0:T(8,128)}, u32[]{:S(2)}) copy-start(f32[10,64,512]{2,1,0:T(8,128)} %get-tuple-element.67) | copy-start | bytes 3932164
  141.9 2.8 copy-start.18
  144.7 21.6 %copy-start.6 = (f32[10,64,512]{2,1,0:T(8,128)}, f32[10,64,512]{2,1,0:T(8,128)S(1)}, u32[]{:S(2)}) copy-start(f32[10,64,512]{2,1,0:T(8,128)S(1)} %subtract_divide_fusion.1) | copy-start | bytes 3932164
  146.6 11.6 %collective-permute-start.12 = (f32[10,1,512]{2,1,0:T(1,128)S(1)}, f32[10,1,512]{2,1,0:T(1,128)S(1)}, u32[]{:S(2)}, u32[]{:S(2)}) collective-permute-start(f32[10,1,512]{2,1,0:T(1,128)S(1)} %get-tuple-element.90), channel_id=1, source_target_pairs={{0,8},{8,16},{16,24},{24,32},{32,40},{40,48},{48,56},{56,64},{64,7... | collective-permute-start | bytes 61448 | tf_op jit(solution)/shard_map/ppermute | solution.py:24
  150.2 8.0 %collective-permute-start.13 = (f32[10,1,512]{2,1,0:T(1,128)S(1)}, f32[10,1,512]{2,1,0:T(1,128)S(1)}, u32[]{:S(2)}, u32[]{:S(2)}) collective-permute-start(f32[10,1,512]{2,1,0:T(1,128)S(1)} %get-tuple-element.91), channel_id=1, source_target_pairs={{8,0},{16,8},{24,16},{32,24},{40,32},{48,40},{56,48},{64,56},{72,6... | collective-permute-start | bytes 61448 | tf_op jit(solution)/shard_map/ppermute | solution.py:25
  153.1 7.6 %collective-permute-start.14 = (f32[10,64,1]{2,1,0:T(8,128)}, f32[10,64,1]{2,1,0:T(8,128)}, u32[]{:S(2)}, u32[]{:S(2)}) collective-permute-start(f32[10,64,1]{2,1,0:T(8,128)} %get-tuple-element.88), channel_id=1, source_target_pairs={{0,1},{1,2},{2,3},{3,4},{4,5},{5,6},{6,7},{8,9},{9,10},{10,11},{11... | collective-permute-start | bytes 7688 | tf_op jit(solution)/shard_map/ppermute | solution.py:24
  155.7 8.7 %collective-permute-start.15 = (f32[10,64,1]{2,1,0:T(8,128)}, f32[10,64,1]{2,1,0:T(8,128)}, u32[]{:S(2)}, u32[]{:S(2)}) collective-permute-start(f32[10,64,1]{2,1,0:T(8,128)} %get-tuple-element.89), channel_id=1, source_target_pairs={{1,0},{2,1},{3,2},{4,3},{5,4},{6,5},{7,6},{9,8},{10,9},{11,10},{12... | collective-permute-start | bytes 7688 | tf_op jit(solution)/shard_map/ppermute | solution.py:25
  158.2 6.2 %copy-start.29 = (f32[10,64,513]{2,1,0:T(8,128)S(1)}, f32[10,64,513]{2,1,0:T(8,128)}, u32[]{:S(2)}) copy-start(f32[10,64,513]{2,1,0:T(8,128)} %get-tuple-element.64) | copy-start | bytes 3939844
  158.2 6.2 %copy-start.30 = (f32[10,64,513]{2,1,0:T(8,128)S(1)}, f32[10,64,513]{2,1,0:T(8,128)}, u32[]{:S(2)}) copy-start(f32[10,64,513]{2,1,0:T(8,128)} %get-tuple-element.65) | copy-start | bytes 3939844
  164.4 2.2 copy-start.33
  207.0 2.4 copy-start.19
  209.8 9.8 %copy-start.2 = (f32[10,64,512]{2,1,0:T(8,128)S(1)}, f32[10,64,512]{2,1,0:T(8,128)}, u32[]{:S(2)}) copy-start(f32[10,64,512]{2,1,0:T(8,128)} %param.8) | copy-start | bytes 3932164
  209.8 9.8 %collective-permute-start.16 = (f32[10,1,512]{2,1,0:T(1,128)S(1)}, f32[10,1,512]{2,1,0:T(1,128)S(1)}, u32[]{:S(2)}, u32[]{:S(2)}) collective-permute-start(f32[10,1,512]{2,1,0:T(1,128)S(1)} %get-tuple-element.86), channel_id=1, source_target_pairs={{0,8},{8,16},{16,24},{24,32},{32,40},{40,48},{48,56},{56,64},{64,7... | collective-permute-start | bytes 61448 | tf_op jit(solution)/shard_map/ppermute | solution.py:24
  213.6 6.0 %collective-permute-start.17 = (f32[10,1,512]{2,1,0:T(1,128)S(1)}, f32[10,1,512]{2,1,0:T(1,128)S(1)}, u32[]{:S(2)}, u32[]{:S(2)}) collective-permute-start(f32[10,1,512]{2,1,0:T(1,128)S(1)} %get-tuple-element.87), channel_id=1, source_target_pairs={{8,0},{16,8},{24,16},{32,24},{40,32},{48,40},{56,48},{64,56},{72,6... | collective-permute-start | bytes 61448 | tf_op jit(solution)/shard_map/ppermute | solution.py:25
  215.1 5.9 %collective-permute-start.18 = (f32[10,64,1]{2,1,0:T(8,128)S(1)}, f32[10,64,1]{2,1,0:T(8,128)S(1)}, u32[]{:S(2)}, u32[]{:S(2)}) collective-permute-start(f32[10,64,1]{2,1,0:T(8,128)S(1)} %get-tuple-element.84), channel_id=1, source_target_pairs={{0,1},{1,2},{2,3},{3,4},{4,5},{5,6},{6,7},{8,9},{9,10},{10,11},{11... | collective-permute-start | bytes 7688 | tf_op jit(solution)/shard_map/ppermute | solution.py:24
  217.0 8.5 %copy-start.23 = (f32[10,64,513]{2,1,0:T(8,128)S(1)}, f32[10,64,513]{2,1,0:T(8,128)}, u32[]{:S(2)}) copy-start(f32[10,64,513]{2,1,0:T(8,128)} %get-tuple-element.71) | copy-start | bytes 3939844
  217.0 8.5 %collective-permute-start.19 = (f32[10,64,1]{2,1,0:T(8,128)S(1)}, f32[10,64,1]{2,1,0:T(8,128)S(1)}, u32[]{:S(2)}, u32[]{:S(2)}) collective-permute-start(f32[10,64,1]{2,1,0:T(8,128)S(1)} %get-tuple-element.85), channel_id=1, source_target_pairs={{1,0},{2,1},{3,2},{4,3},{5,4},{6,5},{7,6},{9,8},{10,9},{11,10},{12... | collective-permute-start | bytes 7688 | tf_op jit(solution)/shard_map/ppermute | solution.py:25
  220.8 6.0 %copy-start.10 = (f32[10,64,512]{2,1,0:T(8,128)S(1)}, f32[10,64,512]{2,1,0:T(8,128)}, u32[]{:S(2)}) copy-start(f32[10,64,512]{2,1,0:T(8,128)} %param.9) | copy-start | bytes 3932164
  220.8 6.0 %copy-start.32 = (f32[10,64,512]{2,1,0:T(8,128)S(1)}, f32[10,64,512]{2,1,0:T(8,128)}, u32[]{:S(2)}) copy-start(f32[10,64,512]{2,1,0:T(8,128)} %param.7) | copy-start | bytes 3932164
  220.9 6.0 %copy-start.43 = (f32[64,512]{1,0:T(8,128)S(1)}, f32[64,512]{1,0:T(8,128)}, u32[]{:S(2)}) copy-start(f32[64,512]{1,0:T(8,128)} %param.10) | copy-start | bytes 393220
  221.0 5.8 %copy-start.38 = (f32[10,64,1]{2,1,0:T(8,128)}, f32[10,64,1]{2,1,0:T(8,128)S(1)}, u32[]{:S(2)}) copy-start(f32[10,64,1]{2,1,0:T(8,128)S(1)} %collective-permute-done.18) | copy-start | bytes 7684
  264.5 10.0 %collective-permute-start.20 = (f32[10,1,512]{2,1,0:T(1,128)S(1)}, f32[10,1,512]{2,1,0:T(1,128)S(1)}, u32[]{:S(2)}, u32[]{:S(2)}) collective-permute-start(f32[10,1,512]{2,1,0:T(1,128)S(1)} %get-tuple-element.82), channel_id=1, source_target_pairs={{0,8},{8,16},{16,24},{24,32},{32,40},{40,48},{48,56},{56,64},{64,7... | collective-permute-start | bytes 61448 | tf_op jit(solution)/shard_map/ppermute | solution.py:24
  268.1 6.4 %collective-permute-start.21 = (f32[10,1,512]{2,1,0:T(1,128)S(1)}, f32[10,1,512]{2,1,0:T(1,128)S(1)}, u32[]{:S(2)}, u32[]{:S(2)}) collective-permute-start(f32[10,1,512]{2,1,0:T(1,128)S(1)} %get-tuple-element.83), channel_id=1, source_target_pairs={{8,0},{16,8},{24,16},{32,24},{40,32},{48,40},{56,48},{64,56},{72,6... | collective-permute-start | bytes 61448 | tf_op jit(solution)/shard_map/ppermute | solution.py:25
  269.6 6.8 %collective-permute-start.22 = (f32[10,64,1]{2,1,0:T(8,128)S(1)}, f32[10,64,1]{2,1,0:T(8,128)S(1)}, u32[]{:S(2)}, u32[]{:S(2)}) collective-permute-start(f32[10,64,1]{2,1,0:T(8,128)S(1)} %get-tuple-element.80), channel_id=1, source_target_pairs={{0,1},{1,2},{2,3},{3,4},{4,5},{5,6},{6,7},{8,9},{9,10},{10,11},{11... | collective-permute-start | bytes 7688 | tf_op jit(solution)/shard_map/ppermute | solution.py:24
  272.2 8.6 %copy-start.24 = (f32[10,64,513]{2,1,0:T(8,128)S(1)}, f32[10,64,513]{2,1,0:T(8,128)}, u32[]{:S(2)}) copy-start(f32[10,64,513]{2,1,0:T(8,128)} %get-tuple-element.71) | copy-start | bytes 3939844
  272.2 8.6 %copy-start.39 = (f32[10,64,1]{2,1,0:T(8,128)S(1)}, f32[10,64,1]{2,1,0:T(8,128)}, u32[]{:S(2)}) copy-start(f32[10,64,1]{2,1,0:T(8,128)} %copy-done.38) | copy-start | bytes 7684
  272.3 8.5 %copy-start.41 = (f32[10,64,1]{2,1,0:T(8,128)S(1)}, f32[10,64,1]{2,1,0:T(8,128)}, u32[]{:S(2)}) copy-start(f32[10,64,1]{2,1,0:T(8,128)} %copy-done.40) | copy-start | bytes 7684
  272.3 8.5 %collective-permute-start.23 = (f32[10,64,1]{2,1,0:T(8,128)S(1)}, f32[10,64,1]{2,1,0:T(8,128)S(1)}, u32[]{:S(2)}, u32[]{:S(2)}) collective-permute-start(f32[10,64,1]{2,1,0:T(8,128)S(1)} %get-tuple-element.81), channel_id=1, source_target_pairs={{1,0},{2,1},{3,2},{4,3},{5,4},{6,5},{7,6},{9,8},{10,9},{11,10},{12... | collective-permute-start | bytes 7688 | tf_op jit(solution)/shard_map/ppermute | solution.py:25
  276.4 7.7 %copy-start.11 = (f32[10,64,512]{2,1,0:T(8,128)S(1)}, f32[10,64,512]{2,1,0:T(8,128)}, u32[]{:S(2)}) copy-start(f32[10,64,512]{2,1,0:T(8,128)} %param.9) | copy-start | bytes 3932164
  276.4 7.7 %copy-start.15 = (f32[10,64,512]{2,1,0:T(8,128)S(1)}, f32[10,64,512]{2,1,0:T(8,128)}, u32[]{:S(2)}) copy-start(f32[10,64,512]{2,1,0:T(8,128)} %get-tuple-element.58) | copy-start | bytes 3932164
  321.3 2.8 copy-start.21
  324.0 6.9 %copy-start.3 = (f32[10,64,512]{2,1,0:T(8,128)}, f32[10,64,512]{2,1,0:T(8,128)S(1)}, u32[]{:S(2)}) copy-start(f32[10,64,512]{2,1,0:T(8,128)S(1)} %subtract_divide_fusion) | copy-start | bytes 3932164
  325.9 11.7 %collective-permute-start.24 = (f32[10,1,512]{2,1,0:T(1,128)S(1)}, f32[10,1,512]{2,1,0:T(1,128)S(1)}, u32[]{:S(2)}, u32[]{:S(2)}) collective-permute-start(f32[10,1,512]{2,1,0:T(1,128)S(1)} %get-tuple-element.78), channel_id=1, source_target_pairs={{0,8},{8,16},{16,24},{24,32},{32,40},{40,48},{48,56},{56,64},{64,7... | collective-permute-start | bytes 61448 | tf_op jit(solution)/shard_map/ppermute | solution.py:24
  329.6 8.1 %collective-permute-start.25 = (f32[10,1,512]{2,1,0:T(1,128)S(1)}, f32[10,1,512]{2,1,0:T(1,128)S(1)}, u32[]{:S(2)}, u32[]{:S(2)}) collective-permute-start(f32[10,1,512]{2,1,0:T(1,128)S(1)} %get-tuple-element.79), channel_id=1, source_target_pairs={{8,0},{16,8},{24,16},{32,24},{40,32},{48,40},{56,48},{64,56},{72,6... | collective-permute-start | bytes 61448 | tf_op jit(solution)/shard_map/ppermute | solution.py:25
  332.6 8.4 %collective-permute-start.26 = (f32[10,64,1]{2,1,0:T(8,128)}, f32[10,64,1]{2,1,0:T(8,128)}, u32[]{:S(2)}, u32[]{:S(2)}) collective-permute-start(f32[10,64,1]{2,1,0:T(8,128)} %get-tuple-element.76), channel_id=1, source_target_pairs={{0,1},{1,2},{2,3},{3,4},{4,5},{5,6},{6,7},{8,9},{9,10},{10,11},{11... | collective-permute-start | bytes 7688 | tf_op jit(solution)/shard_map/ppermute | solution.py:24
  334.5 8.7 %collective-permute-start.27 = (f32[10,64,1]{2,1,0:T(8,128)}, f32[10,64,1]{2,1,0:T(8,128)}, u32[]{:S(2)}, u32[]{:S(2)}) collective-permute-start(f32[10,64,1]{2,1,0:T(8,128)} %get-tuple-element.77), channel_id=1, source_target_pairs={{1,0},{2,1},{3,2},{4,3},{5,4},{6,5},{7,6},{9,8},{10,9},{11,10},{12... | collective-permute-start | bytes 7688 | tf_op jit(solution)/shard_map/ppermute | solution.py:25
  337.7 5.6 %copy-start.4 = (f32[10,64,512]{2,1,0:T(8,128)S(1)}, f32[10,64,512]{2,1,0:T(8,128)}, u32[]{:S(2)}) copy-start(f32[10,64,512]{2,1,0:T(8,128)} %copy-done.3) | copy-start | bytes 3932164
  337.7 5.6 %copy-start.27 = (f32[10,64,513]{2,1,0:T(8,128)S(1)}, f32[10,64,513]{2,1,0:T(8,128)}, u32[]{:S(2)}) copy-start(f32[10,64,513]{2,1,0:T(8,128)} %get-tuple-element.55) | copy-start | bytes 3939844
  337.7 5.6 %copy-start.28 = (f32[10,64,513]{2,1,0:T(8,128)S(1)}, f32[10,64,513]{2,1,0:T(8,128)}, u32[]{:S(2)}) copy-start(f32[10,64,513]{2,1,0:T(8,128)} %get-tuple-element.56) | copy-start | bytes 3939844
  345.5 39.8 %copy-start.5 = (f32[10,64,512]{2,1,0:T(8,128)S(1)}, f32[10,64,512]{2,1,0:T(8,128)}, u32[]{:S(2)}) copy-start(f32[10,64,512]{2,1,0:T(8,128)} %copy-done.3) | copy-start | bytes 3932164
  (9 other events, 15.9 us)
where the time goes:
time: 392 us; the launch traced here: 390 us
  blocking collectives  198 us (51%)
  other arithmetic  74.3 us (19%)
  starting transfers between devices  71.2 us (18%)
  between operations  19.5 us (5%)
  waiting for transfers between devices  17.5 us (4%)
  local copies, waits for them, and re-layouts  8.9 us (2%)
    psum x24, blocking collectives, by_axis(): value = lax.psum(value, axis)  198 us
    ppermute x14, starting transfers between devices, padded(): lax.ppermute(last, axis, up)  45.4 us
    ppermute x14, starting transfers between devices, padded(): lax.ppermute(initial, axis, [(b, a) for a, b in up])  25.8 us
    ppermute x14, waiting for transfers between devices, padded(): lax.ppermute(initial, axis, [(b, a) for a, b in up])  17.3 us
    add x4, other arithmetic, jacobian_apply(): flow_y = y_low * vector[:, 1:-1, :-1] + y_high * vector[:, 1:-1, 1:]  11.4 us
    mul x6, other arithmetic, face_pair(): return (coef_low, coef_high, transmit * mobility * head_drop)  10.8 us
    add x4, other arithmetic, jacobian_apply(): flow_x = x_low * vector[:, :-1, 1:-1] + x_high * vector[:, 1:, 1:-1]  10.7 us
  transfers between devices with their start and end apart: 28, of which 7 were waited for; matrix products, arithmetic and copies ran while one was open for 6% of the time, Pallas kernels for 0%

commit v1 on v0

--- a/solution.py
+++ b/solution.py
@@ -35,7 +35,7 @@
 
 def by_axis(value, axes):
     for axis in axes:
-        value = lax.psum(value, axis)
+        value = jnp.sum(lax.all_gather(value, axis), axis=0)
     return value
 
 

time: 392 us -> 488 us (1.24); the launches traced: 390 us -> 479 us
  local copies, waits for them, and re-layouts: 8.9 us -> 83.8 us
  other arithmetic: 74.3 us -> 104 us
  blocking collectives: 198 us -> 182 us
    psum x24 -> x0, blocking collectives: 198 us -> none  [by_axis(): value = lax.psum(value, axis)]
    unnamed x0 -> x24, blocking collectives: none -> 182 us
    unnamed x91 -> x199, local copies, waits for them, and re-layouts: 2.73 us -> 75.1 us
    reduce_sum x0 -> x48, other arithmetic: none -> 31.3 us  [by_axis(): value = jnp.sum(lax.all_gather(value, axis), axis=0)]
where the time goes in v1:
time: 488 us; the launch traced here: 479 us
  blocking collectives  182 us (37%)
  other arithmetic  104 us (21%)
  local copies, waits for them, and re-layouts  83.8 us (17%)
  starting transfers between devices  70.4 us (14%)
  between operations  20.2 us (4%)
  waiting for transfers between devices  18.5 us (4%)
    unnamed x24, blocking collectives  182 us
    unnamed x199, local copies, waits for them, and re-layouts  75.1 us
    ppermute x14, starting transfers between devices, padded(): lax.ppermute(last, axis, up)  45.3 us
    reduce_sum x48, other arithmetic, by_axis(): value = jnp.sum(lax.all_gather(value, axis), axis=0)  31.3 us
    ppermute x14, starting transfers between devices, padded(): lax.ppermute(initial, axis, [(b, a) for a, b in up])  25.1 us
    ppermute x14, waiting for transfers between devices, padded(): lax.ppermute(initial, axis, [(b, a) for a, b in up])  18.3 us
    mul x6, other arithmetic, face_pair(): return (coef_low, coef_high, transmit * mobility * head_drop)  10.8 us
    add x4, other arithmetic, jacobian_apply(): flow_x = x_low * vector[:, :-1, 1:-1] + x_high * vector[:, 1:, 1:-1]  10.5 us
  transfers between devices with their start and end apart: 28, of which 7 were waited for; matrix products, arithmetic and copies ran while one was open for 6% of the time, Pallas kernels for 0%

profile of v1, /device:TPU:1, one launch (start us, length us, event | category | flops | bytes accessed | tf_op | source)
XLA Modules:
  0.0 479.3 jit_solution(8946434409775386232)
XLA Ops:
  3.4 3.9 collective-permute-start
  9.8 4.0 collective-permute-start.2
  13.8 1.9 collective-permute-start.3
  20.4 4.9 %collective-permute-start.4 = (f32[10,1,512]{2,1,0:T(1,128)S(1)}, f32[10,1,512]{2,1,0:T(1,128)S(1)}, u32[]{:S(2)}, u32[]{:S(2)}) collective-permute-start(f32[10,1,512]{2,1,0:T(1,128)S(1)} %get-tuple-element.98), channel_id=1, source_target_pairs={{0,8},{8,16},{16,24},{24,32},{32,40},{40,48},{48,56},{56,64},{64,7... | collective-permute-start | bytes 61448 | tf_op jit(solution)/shard_map/ppermute | solution.py:24
  26.4 3.9 collective-permute-start.6
  32.1 1.9 collective-permute-start.7
  40.8 5.1 %multiply_multiply_fusion.1 = (f32[10,64,513]{2,1,0:T(8,128)S(1)}, f32[10,64,513]{2,1,0:T(8,128)}) fusion(f32[10,64,1]{2,1,0:T(8,128)} %collective-permute-done.7, f32[10,1,512]{2,1,0:T(1,128)S(1)} %collective-permute-done.5, f32[10,64,512]{2,1,0:T(8,128)S(1)} %copy-done, f32[10,1,512]{2,1,0:T(1,128)S(1)} %collective-permute-done.4, ...), kind=kLoop, calls=%fused_computation.83 | loop fusion | flops 11162880 | bytes 5738672 | tf_op jit(solution)/shard_map/mul | solution.py:63
  46.0 2.9 multiply_reduce_fusion.11
  50.9 12.4 %all-reduce.27 = f32[4]{0:T(128)S(1)} all-reduce(f32[4]{0:T(128)S(1)} %dynamic-update-slice), channel_id=1, replica_groups=mesh['gx_0'=4,'gx_1'=4,'gy_0'=4,'gy_1'=2] {'gx_0'}, use_global_device_ids=true, to_apply=%add.27 | all-reduce | flops 4 | bytes 32
  66.0 6.6 %all-reduce.28 = f32[4]{0:T(128)S(1)} all-reduce(f32[4]{0:T(128)S(1)} %dynamic-update-slice.1), channel_id=1, replica_groups=mesh['gx_0'=4,'gx_1'=4,'gy_0'=4,'gy_1'=2] {'gx_1'}, use_global_device_ids=true, to_apply=%add.28 | all-reduce | flops 4 | bytes 32
  75.2 7.0 %all-reduce.29 = f32[4]{0:T(128)S(1)} all-reduce(f32[4]{0:T(128)S(1)} %dynamic-update-slice.2), channel_id=1, replica_groups=mesh['gx_0'=4,'gx_1'=4,'gy_0'=4,'gy_1'=2] {'gy_0'}, use_global_device_ids=true, to_apply=%add.29 | all-reduce | flops 4 | bytes 32
  84.1 9.2 %all-reduce.30 = f32[2]{0:T(128)S(1)} all-reduce(f32[2]{0:T(128)S(1)} %dynamic-update-slice.3), channel_id=1, replica_groups=mesh['gx_0'=4,'gx_1'=4,'gy_0'=4,'gy_1'=2] {'gy_1'}, use_global_device_ids=true, to_apply=%add.30 | all-reduce | flops 2 | bytes 16
  96.4 3.0 collective-permute-start.8
  100.7 1.9 collective-permute-start.10
  102.7 2.9 collective-permute-start.11
  106.9 3.0 fusion.30
  111.1 4.4 fusion.19
  115.5 2.9 multiply_reduce_fusion.10
  121.2 10.1 %all-reduce.86 = (f32[4]{0:T(128)S(1)}, f32[4]{0:T(128)S(1)}) all-reduce(f32[4]{0:T(128)S(1)} %dynamic-update-slice.8, f32[4]{0:T(128)S(1)} %dynamic-update-slice.4), channel_id=1, replica_groups=mesh['gx_0'=4,'gx_1'=4,'gy_0'=4,'gy_1'=2] {'gx_0'}, use_global_device_ids=true, to_apply=%add.35 | all-reduce | flops 8 | bytes 64
  135.6 6.0 %all-reduce.82 = (f32[4]{0:T(128)S(1)}, f32[4]{0:T(128)S(1)}) all-reduce(f32[4]{0:T(128)S(1)} %dynamic-update-slice.9, f32[4]{0:T(128)S(1)} %dynamic-update-slice.5), channel_id=1, replica_groups=mesh['gx_0'=4,'gx_1'=4,'gy_0'=4,'gy_1'=2] {'gx_1'}, use_global_device_ids=true, to_apply=%add.36 | all-reduce | flops 8 | bytes 64
  145.9 6.9 %all-reduce.78 = (f32[4]{0:T(128)S(1)}, f32[4]{0:T(128)S(1)}) all-reduce(f32[4]{0:T(128)S(1)} %dynamic-update-slice.10, f32[4]{0:T(128)S(1)} %dynamic-update-slice.6), channel_id=1, replica_groups=mesh['gx_0'=4,'gx_1'=4,'gy_0'=4,'gy_1'=2] {'gy_0'}, use_global_device_ids=true, to_apply=%add.37 | all-reduce | flops 8 | bytes 64
  157.0 7.3 %all-reduce.90 = (f32[2]{0:T(128)S(1)}, f32[2]{0:T(128)S(1)}) all-reduce(f32[2]{0:T(128)S(1)} %dynamic-update-slice.11, f32[2]{0:T(128)S(1)} %dynamic-update-slice.7), channel_id=1, replica_groups=mesh['gx_0'=4,'gx_1'=4,'gy_0'=4,'gy_1'=2] {'gy_1'}, use_global_device_ids=true, to_apply=%add.38 | all-reduce | flops 4 | bytes 32
  167.6 2.8 subtract_divide_fusion.1
  172.3 3.6 collective-permute-start.12
  178.1 2.6 collective-permute-start.14
  180.7 1.9 collective-permute-start.15
  182.7 2.5 fusion.31
  185.2 4.1 collective-permute-done.15
  191.4 2.0 multiply_reduce_fusion.6
  197.5 9.3 %all-reduce.85 = (f32[4]{0:T(128)S(1)}, f32[4]{0:T(128)S(1)}, f32[4]{0:T(128)S(1)}) all-reduce(f32[4]{0:T(128)S(1)} %dynamic-update-slice.16, f32[4]{0:T(128)S(1)} %dynamic-update-slice.12, f32[4]{0:T(128)S(1)} %dynamic-update-slice.20), channel_id=1, replica_groups=mesh['gx_0'=4,'gx_1'=4,'gy_0'=4,'gy_1'=2] {'gx_0'}, use_global_device_ids=true, to_apply=%add.43 | all-reduce | flops 12 | bytes 96
  213.2 6.0 %all-reduce.81 = (f32[4]{0:T(128)S(1)}, f32[4]{0:T(128)S(1)}, f32[4]{0:T(128)S(1)}) all-reduce(f32[4]{0:T(128)S(1)} %dynamic-update-slice.17, f32[4]{0:T(128)S(1)} %dynamic-update-slice.13, f32[4]{0:T(128)S(1)} %dynamic-update-slice.21), channel_id=1, replica_groups=mesh['gx_0'=4,'gx_1'=4,'gy_0'=4,'gy_1'=2] {'gx_1'}, use_global_device_ids=true, to_apply=%add.44 | all-reduce | flops 12 | bytes 96
  226.5 6.0 %all-reduce.77 = (f32[4]{0:T(128)S(1)}, f32[4]{0:T(128)S(1)}, f32[4]{0:T(128)S(1)}) all-reduce(f32[4]{0:T(128)S(1)} %dynamic-update-slice.18, f32[4]{0:T(128)S(1)} %dynamic-update-slice.14, f32[4]{0:T(128)S(1)} %dynamic-update-slice.22), channel_id=1, replica_groups=mesh['gx_0'=4,'gx_1'=4,'gy_0'=4,'gy_1'=2] {'gy_0'}, use_global_device_ids=true, to_apply=%add.45 | all-reduce | flops 12 | bytes 96
  238.6 7.9 %all-reduce.89 = (f32[2]{0:T(128)S(1)}, f32[2]{0:T(128)S(1)}, f32[2]{0:T(128)S(1)}) all-reduce(f32[2]{0:T(128)S(1)} %dynamic-update-slice.19, f32[2]{0:T(128)S(1)} %dynamic-update-slice.15, f32[2]{0:T(128)S(1)} %dynamic-update-slice.23), channel_id=1, replica_groups=mesh['gx_0'=4,'gx_1'=4,'gy_0'=4,'gy_1'=2] {'gy_1'}, use_global_device_ids=true, to_apply=%add.46 | all-reduce | flops 6 | bytes 48
  254.4 2.3 add_add_fusion.1
  257.2 3.8 collective-permute-start.16
  262.5 1.9 collective-permute-start.18
  264.4 2.6 collective-permute-start.19
  268.4 4.5 collective-permute-done.19
  274.2 3.0 multiply_reduce_fusion.5
  278.7 9.5 %all-reduce.51 = f32[4]{0:T(128)S(1)} all-reduce(f32[4]{0:T(128)S(1)} %dynamic-update-slice.24), channel_id=1, replica_groups=mesh['gx_0'=4,'gx_1'=4,'gy_0'=4,'gy_1'=2] {'gx_0'}, use_global_device_ids=true, to_apply=%add.51 | all-reduce | flops 4 | bytes 32
  290.3 6.0 %all-reduce.52 = f32[4]{0:T(128)S(1)} all-reduce(f32[4]{0:T(128)S(1)} %dynamic-update-slice.25), channel_id=1, replica_groups=mesh['gx_0'=4,'gx_1'=4,'gy_0'=4,'gy_1'=2] {'gx_1'}, use_global_device_ids=true, to_apply=%add.52 | all-reduce | flops 4 | bytes 32
  298.4 6.8 %all-reduce.53 = f32[4]{0:T(128)S(1)} all-reduce(f32[4]{0:T(128)S(1)} %dynamic-update-slice.26), channel_id=1, replica_groups=mesh['gx_0'=4,'gx_1'=4,'gy_0'=4,'gy_1'=2] {'gy_0'}, use_global_device_ids=true, to_apply=%add.53 | all-reduce | flops 4 | bytes 32
  307.2 7.0 %all-reduce.54 = f32[2]{0:T(128)S(1)} all-reduce(f32[2]{0:T(128)S(1)} %dynamic-update-slice.27), channel_id=1, replica_groups=mesh['gx_0'=4,'gx_1'=4,'gy_0'=4,'gy_1'=2] {'gy_1'}, use_global_device_ids=true, to_apply=%add.54 | all-reduce | flops 2 | bytes 16
  318.2 3.6 collective-permute-start.20
  323.3 2.6 collective-permute-start.22
  325.9 2.1 collective-permute-start.23
  329.9 4.6 collective-permute-done.23
  334.5 3.3 fusion.7
  337.8 2.9 multiply_reduce_fusion.4
  343.4 9.2 %all-reduce.84 = (f32[4]{0:T(128)S(1)}, f32[4]{0:T(128)S(1)}) all-reduce(f32[4]{0:T(128)S(1)} %dynamic-update-slice.32, f32[4]{0:T(128)S(1)} %dynamic-update-slice.28), channel_id=1, replica_groups=mesh['gx_0'=4,'gx_1'=4,'gy_0'=4,'gy_1'=2] {'gx_0'}, use_global_device_ids=true, to_apply=%add.59 | all-reduce | flops 8 | bytes 64
  357.2 6.0 %all-reduce.80 = (f32[4]{0:T(128)S(1)}, f32[4]{0:T(128)S(1)}) all-reduce(f32[4]{0:T(128)S(1)} %dynamic-update-slice.33, f32[4]{0:T(128)S(1)} %dynamic-update-slice.29), channel_id=1, replica_groups=mesh['gx_0'=4,'gx_1'=4,'gy_0'=4,'gy_1'=2] {'gx_1'}, use_global_device_ids=true, to_apply=%add.60 | all-reduce | flops 8 | bytes 64
  367.5 6.0 %all-reduce.76 = (f32[4]{0:T(128)S(1)}, f32[4]{0:T(128)S(1)}) all-reduce(f32[4]{0:T(128)S(1)} %dynamic-update-slice.34, f32[4]{0:T(128)S(1)} %dynamic-update-slice.30), channel_id=1, replica_groups=mesh['gx_0'=4,'gx_1'=4,'gy_0'=4,'gy_1'=2] {'gy_0'}, use_global_device_ids=true, to_apply=%add.61 | all-reduce | flops 8 | bytes 64
  377.6 7.7 %all-reduce.88 = (f32[2]{0:T(128)S(1)}, f32[2]{0:T(128)S(1)}) all-reduce(f32[2]{0:T(128)S(1)} %dynamic-update-slice.35, f32[2]{0:T(128)S(1)} %dynamic-update-slice.31), channel_id=1, replica_groups=mesh['gx_0'=4,'gx_1'=4,'gy_0'=4,'gy_1'=2] {'gy_1'}, use_global_device_ids=true, to_apply=%add.62 | all-reduce | flops 4 | bytes 32
  388.3 2.7 subtract_divide_fusion
  392.9 3.6 collective-permute-start.24
  400.7 2.7 collective-permute-start.27
  403.4 3.2 fusion.33
  406.6 3.0 collective-permute-done.27
  411.7 3.0 multiply_reduce_fusion
  418.8 9.5 %all-reduce.83 = (f32[4]{0:T(128)S(1)}, f32[4]{0:T(128)S(1)}, f32[4]{0:T(128)S(1)}) all-reduce(f32[4]{0:T(128)S(1)} %dynamic-update-slice.40, f32[4]{0:T(128)S(1)} %dynamic-update-slice.36, f32[4]{0:T(128)S(1)} %dynamic-update-slice.44), channel_id=1, replica_groups=mesh['gx_0'=4,'gx_1'=4,'gy_0'=4,'gy_1'=2] {'gx_0'}, use_global_device_ids=true, to_apply=%add.67 | all-reduce | flops 12 | bytes 96
  434.5 6.0 %all-reduce.79 = (f32[4]{0:T(128)S(1)}, f32[4]{0:T(128)S(1)}, f32[4]{0:T(128)S(1)}) all-reduce(f32[4]{0:T(128)S(1)} %dynamic-update-slice.41, f32[4]{0:T(128)S(1)} %dynamic-update-slice.37, f32[4]{0:T(128)S(1)} %dynamic-update-slice.45), channel_id=1, replica_groups=mesh['gx_0'=4,'gx_1'=4,'gy_0'=4,'gy_1'=2] {'gx_1'}, use_global_device_ids=true, to_apply=%add.68 | all-reduce | flops 12 | bytes 96
  447.3 6.8 %all-reduce.75 = (f32[4]{0:T(128)S(1)}, f32[4]{0:T(128)S(1)}, f32[4]{0:T(128)S(1)}) all-reduce(f32[4]{0:T(128)S(1)} %dynamic-update-slice.42, f32[4]{0:T(128)S(1)} %dynamic-update-slice.38, f32[4]{0:T(128)S(1)} %dynamic-update-slice.46), channel_id=1, replica_groups=mesh['gx_0'=4,'gx_1'=4,'gy_0'=4,'gy_1'=2] {'gy_0'}, use_global_device_ids=true, to_apply=%add.69 | all-reduce | flops 12 | bytes 96
  459.9 7.1 %all-reduce.87 = (f32[2]{0:T(128)S(1)}, f32[2]{0:T(128)S(1)}, f32[2]{0:T(128)S(1)}) all-reduce(f32[2]{0:T(128)S(1)} %dynamic-update-slice.43, f32[2]{0:T(128)S(1)} %dynamic-update-slice.39, f32[2]{0:T(128)S(1)} %dynamic-update-slice.47), channel_id=1, replica_groups=mesh['gx_0'=4,'gx_1'=4,'gy_0'=4,'gy_1'=2] {'gy_1'}, use_global_device_ids=true, to_apply=%add.70 | all-reduce | flops 6 | bytes 48
  474.7 4.4 multiply_subtract_fusion
  (316 shorter events, 150.6 us)
Async XLA Ops:
  0.6 8.2 %copy-start.1 = (f32[10,64,512]{2,1,0:T(8,128)S(1)}, f32[10,64,512]{2,1,0:T(8,128)}, u32[]{:S(2)}) copy-start(f32[10,64,512]{2,1,0:T(8,128)} %param.8) | copy-start | bytes 3932164
  1.7 14.1 %copy-start = (f32[10,64,512]{2,1,0:T(8,128)S(1)}, f32[10,64,512]{2,1,0:T(8,128)}, u32[]{:S(2)}) copy-start(f32[10,64,512]{2,1,0:T(8,128)} %param.6) | copy-start | bytes 3932164
  3.4 32.2 %collective-permute-start = (f32[11,1,512]{2,1,0:T(1,128)}, f32[11,1,512]{2,1,0:T(1,128)S(1)}, u32[]{:S(2)}, u32[]{:S(2)}) collective-permute-start(f32[11,1,512]{2,1,0:T(1,128)} %get-tuple-element.72), channel_id=1, source_target_pairs={{0,8},{8,16},{16,24},{24,32},{32,40},{40,48},{48,56},{56,64},{64,7... | collective-permute-start | bytes 67592 | tf_op jit(solution)/shard_map/ppermute | solution.py:24
  7.4 11.3 %copy-start.44 = (s32[64,512]{1,0:T(8,128)S(1)}, s32[64,512]{1,0:T(8,128)}, u32[]{:S(2)}) copy-start(s32[64,512]{1,0:T(8,128)} %param.11) | copy-start | bytes 393220
  7.4 28.3 %collective-permute-start.1 = (f32[11,1,512]{2,1,0:T(1,128)S(1)}, f32[11,1,512]{2,1,0:T(1,128)S(1)}, u32[]{:S(2)}, u32[]{:S(2)}) collective-permute-start(f32[11,1,512]{2,1,0:T(1,128)S(1)} %get-tuple-element.73), channel_id=1, source_target_pairs={{8,0},{16,8},{24,16},{32,24},{40,32},{48,40},{56,48},{64,56},{72,6... | collective-permute-start | bytes 67592 | tf_op jit(solution)/shard_map/ppermute | solution.py:25
  9.8 10.6 %collective-permute-start.2 = (f32[11,64,1]{2,1,0:T(8,128)}, f32[11,64,1]{2,1,0:T(8,128)}, u32[]{:S(2)}, u32[]{:S(2)}) collective-permute-start(f32[11,64,1]{2,1,0:T(8,128)} %get-tuple-element.74), channel_id=1, source_target_pairs={{0,1},{1,2},{2,3},{3,4},{4,5},{5,6},{6,7},{8,9},{9,10},{10,11},{11... | collective-permute-start | bytes 8456 | tf_op jit(solution)/shard_map/ppermute | solution.py:24
  13.8 12.5 %collective-permute-start.3 = (f32[11,64,1]{2,1,0:T(8,128)}, f32[11,64,1]{2,1,0:T(8,128)}, u32[]{:S(2)}, u32[]{:S(2)}) collective-permute-start(f32[11,64,1]{2,1,0:T(8,128)} %get-tuple-element.75), channel_id=1, source_target_pairs={{1,0},{2,1},{3,2},{4,3},{5,4},{6,5},{7,6},{9,8},{10,9},{11,10},{12... | collective-permute-start | bytes 8456 | tf_op jit(solution)/shard_map/ppermute | solution.py:25
  16.4 15.7 %collective-permute-start.5 = (f32[10,1,512]{2,1,0:T(1,128)}, f32[10,1,512]{2,1,0:T(1,128)S(1)}, u32[]{:S(2)}, u32[]{:S(2)}) collective-permute-start(f32[10,1,512]{2,1,0:T(1,128)} %get-tuple-element.99), channel_id=1, source_target_pairs={{8,0},{16,8},{24,16},{32,24},{40,32},{48,40},{56,48},{64,56},{72,6... | collective-permute-start | bytes 61448 | tf_op jit(solution)/shard_map/ppermute | solution.py:25
  20.4 18.1 %collective-permute-start.4 = (f32[10,1,512]{2,1,0:T(1,128)S(1)}, f32[10,1,512]{2,1,0:T(1,128)S(1)}, u32[]{:S(2)}, u32[]{:S(2)}) collective-permute-start(f32[10,1,512]{2,1,0:T(1,128)S(1)} %get-tuple-element.98), channel_id=1, source_target_pairs={{0,8},{8,16},{16,24},{24,32},{32,40},{40,48},{48,56},{56,64},{64,7... | collective-permute-start | bytes 61448 | tf_op jit(solution)/shard_map/ppermute | solution.py:24
  26.3 10.2 %copy-start.35 = (f32[11,66,1]{2,1,0:T(8,128)}, f32[11,66,1]{2,1,0:T(8,128)S(1)}, u32[]{:S(2)}) copy-start(f32[11,66,1]{2,1,0:T(8,128)S(1)} %pad.57) | copy-start | bytes 8716
  26.4 13.4 %collective-permute-start.6 = (f32[10,64,1]{2,1,0:T(8,128)}, f32[10,64,1]{2,1,0:T(8,128)}, u32[]{:S(2)}, u32[]{:S(2)}) collective-permute-start(f32[10,64,1]{2,1,0:T(8,128)} %get-tuple-element.96), channel_id=1, source_target_pairs={{0,1},{1,2},{2,3},{3,4},{4,5},{5,6},{6,7},{8,9},{9,10},{10,11},{11... | collective-permute-start | bytes 7688 | tf_op jit(solution)/shard_map/ppermute | solution.py:24
  32.1 8.7 %collective-permute-start.7 = (f32[10,64,1]{2,1,0:T(8,128)}, f32[10,64,1]{2,1,0:T(8,128)}, u32[]{:S(2)}, u32[]{:S(2)}) collective-permute-start(f32[10,64,1]{2,1,0:T(8,128)} %get-tuple-element.97), channel_id=1, source_target_pairs={{1,0},{2,1},{3,2},{4,3},{5,4},{6,5},{7,6},{9,8},{10,9},{11,10},{12... | collective-permute-start | bytes 7688 | tf_op jit(solution)/shard_map/ppermute | solution.py:25
  40.8 5.2 %copy-start.7 = (f32[10,64,512]{2,1,0:T(8,128)S(1)}, f32[10,64,512]{2,1,0:T(8,128)}, u32[]{:S(2)}) copy-start(f32[10,64,512]{2,1,0:T(8,128)} %param.9) | copy-start | bytes 3932164
  40.8 5.2 %copy-start.31 = (f32[10,64,512]{2,1,0:T(8,128)S(1)}, f32[10,64,512]{2,1,0:T(8,128)}, u32[]{:S(2)}) copy-start(f32[10,64,512]{2,1,0:T(8,128)} %param.7) | copy-start | bytes 3932164
  40.8 5.2 %copy-start.42 = (f32[64,512]{1,0:T(8,128)S(1)}, f32[64,512]{1,0:T(8,128)}, u32[]{:S(2)}) copy-start(f32[64,512]{1,0:T(8,128)} %param.10) | copy-start | bytes 393220
  45.9 4.3 copy-start.47
  46.0 19.4 %copy-start.46 = (u32[128]{0:T(128)S(1)}, u32[128]{0:T(128)}, u32[]{:S(2)}) copy-start(u32[128]{0:T(128)} %constant.89) | copy-start | bytes 1540
  46.0 28.6 %copy-start.45 = (u32[128]{0:T(128)S(1)}, u32[128]{0:T(128)}, u32[]{:S(2)}) copy-start(u32[128]{0:T(128)} %constant.94) | copy-start | bytes 1540
  94.6 10.9 %copy-start.17 = (f32[9,64,512]{2,1,0:T(8,128)S(1)}, f32[9,64,512]{2,1,0:T(8,128)}, u32[]{:S(2)}) copy-start(f32[9,64,512]{2,1,0:T(8,128)} %get-tuple-element.69) | copy-start | bytes 3538948
  96.4 10.0 %collective-permute-start.8 = (f32[10,1,512]{2,1,0:T(1,128)S(1)}, f32[10,1,512]{2,1,0:T(1,128)S(1)}, u32[]{:S(2)}, u32[]{:S(2)}) collective-permute-start(f32[10,1,512]{2,1,0:T(1,128)S(1)} %get-tuple-element.94), channel_id=1, source_target_pairs={{0,8},{8,16},{16,24},{24,32},{32,40},{40,48},{48,56},{56,64},{64,7... | collective-permute-start | bytes 61448 | tf_op jit(solution)/shard_map/ppermute | solution.py:24
  99.4 7.0 %collective-permute-start.9 = (f32[10,1,512]{2,1,0:T(1,128)S(1)}, f32[10,1,512]{2,1,0:T(1,128)S(1)}, u32[]{:S(2)}, u32[]{:S(2)}) collective-permute-start(f32[10,1,512]{2,1,0:T(1,128)S(1)} %get-tuple-element.95), channel_id=1, source_target_pairs={{8,0},{16,8},{24,16},{32,24},{40,32},{48,40},{56,48},{64,56},{72,6... | collective-permute-start | bytes 61448 | tf_op jit(solution)/shard_map/ppermute | solution.py:25
  100.7 9.2 %collective-permute-start.10 = (f32[10,64,1]{2,1,0:T(8,128)S(1)}, f32[10,64,1]{2,1,0:T(8,128)S(1)}, u32[]{:S(2)}, u32[]{:S(2)}) collective-permute-start(f32[10,64,1]{2,1,0:T(8,128)S(1)} %get-tuple-element.92), channel_id=1, source_target_pairs={{0,1},{1,2},{2,3},{3,4},{4,5},{5,6},{6,7},{8,9},{9,10},{10,11},{11... | collective-permute-start | bytes 7688 | tf_op jit(solution)/shard_map/ppermute | solution.py:24
  102.7 8.4 %collective-permute-start.11 = (f32[10,64,1]{2,1,0:T(8,128)S(1)}, f32[10,64,1]{2,1,0:T(8,128)S(1)}, u32[]{:S(2)}, u32[]{:S(2)}) collective-permute-start(f32[10,64,1]{2,1,0:T(8,128)S(1)} %get-tuple-element.93), channel_id=1, source_target_pairs={{1,0},{2,1},{3,2},{4,3},{5,4},{6,5},{7,6},{9,8},{10,9},{11,10},{12... | collective-permute-start | bytes 7688 | tf_op jit(solution)/shard_map/ppermute | solution.py:25
  106.4 4.7 copy-start.22
  111.1 4.4 copy-start.8
  111.1 4.4 copy-start.13
  167.6 2.9 copy-start.18
  170.4 19.6 %copy-start.6 = (f32[10,64,512]{2,1,0:T(8,128)}, f32[10,64,512]{2,1,0:T(8,128)S(1)}, u32[]{:S(2)}) copy-start(f32[10,64,512]{2,1,0:T(8,128)S(1)} %subtract_divide_fusion.1) | copy-start | bytes 3932164
  172.3 10.4 %collective-permute-start.12 = (f32[10,1,512]{2,1,0:T(1,128)S(1)}, f32[10,1,512]{2,1,0:T(1,128)S(1)}, u32[]{:S(2)}, u32[]{:S(2)}) collective-permute-start(f32[10,1,512]{2,1,0:T(1,128)S(1)} %get-tuple-element.90), channel_id=1, source_target_pairs={{0,8},{8,16},{16,24},{24,32},{32,40},{40,48},{48,56},{56,64},{64,7... | collective-permute-start | bytes 61448 | tf_op jit(solution)/shard_map/ppermute | solution.py:24
  175.9 6.8 %collective-permute-start.13 = (f32[10,1,512]{2,1,0:T(1,128)S(1)}, f32[10,1,512]{2,1,0:T(1,128)S(1)}, u32[]{:S(2)}, u32[]{:S(2)}) collective-permute-start(f32[10,1,512]{2,1,0:T(1,128)S(1)} %get-tuple-element.91), channel_id=1, source_target_pairs={{8,0},{16,8},{24,16},{32,24},{40,32},{48,40},{56,48},{64,56},{72,6... | collective-permute-start | bytes 61448 | tf_op jit(solution)/shard_map/ppermute | solution.py:25
  178.1 7.1 %collective-permute-start.14 = (f32[10,64,1]{2,1,0:T(8,128)}, f32[10,64,1]{2,1,0:T(8,128)S(1)}, u32[]{:S(2)}, u32[]{:S(2)}) collective-permute-start(f32[10,64,1]{2,1,0:T(8,128)} %get-tuple-element.88), channel_id=1, source_target_pairs={{0,1},{1,2},{2,3},{3,4},{4,5},{5,6},{6,7},{8,9},{9,10},{10,11},{11... | collective-permute-start | bytes 7688 | tf_op jit(solution)/shard_map/ppermute | solution.py:24
  180.7 8.6 %collective-permute-start.15 = (f32[10,64,1]{2,1,0:T(8,128)}, f32[10,64,1]{2,1,0:T(8,128)S(1)}, u32[]{:S(2)}, u32[]{:S(2)}) collective-permute-start(f32[10,64,1]{2,1,0:T(8,128)} %get-tuple-element.89), channel_id=1, source_target_pairs={{1,0},{2,1},{3,2},{4,3},{5,4},{6,5},{7,6},{9,8},{10,9},{11,10},{12... | collective-permute-start | bytes 7688 | tf_op jit(solution)/shard_map/ppermute | solution.py:25
  182.7 6.7 %copy-start.29 = (f32[10,64,513]{2,1,0:T(8,128)S(1)}, f32[10,64,513]{2,1,0:T(8,128)}, u32[]{:S(2)}) copy-start(f32[10,64,513]{2,1,0:T(8,128)} %get-tuple-element.64) | copy-start | bytes 3939844
  182.7 6.7 %copy-start.30 = (f32[10,64,513]{2,1,0:T(8,128)S(1)}, f32[10,64,513]{2,1,0:T(8,128)}, u32[]{:S(2)}) copy-start(f32[10,64,513]{2,1,0:T(8,128)} %get-tuple-element.65) | copy-start | bytes 3939844
  254.4 2.4 copy-start.19
  257.2 9.8 %copy-start.2 = (f32[10,64,512]{2,1,0:T(8,128)S(1)}, f32[10,64,512]{2,1,0:T(8,128)}, u32[]{:S(2)}) copy-start(f32[10,64,512]{2,1,0:T(8,128)} %param.8) | copy-start | bytes 3932164
  257.2 9.8 %collective-permute-start.16 = (f32[10,1,512]{2,1,0:T(1,128)S(1)}, f32[10,1,512]{2,1,0:T(1,128)S(1)}, u32[]{:S(2)}, u32[]{:S(2)}) collective-permute-start(f32[10,1,512]{2,1,0:T(1,128)S(1)} %get-tuple-element.86), channel_id=1, source_target_pairs={{0,8},{8,16},{16,24},{24,32},{32,40},{40,48},{48,56},{56,64},{64,7... | collective-permute-start | bytes 61448 | tf_op jit(solution)/shard_map/ppermute | solution.py:24
  261.0 6.0 %collective-permute-start.17 = (f32[10,1,512]{2,1,0:T(1,128)S(1)}, f32[10,1,512]{2,1,0:T(1,128)S(1)}, u32[]{:S(2)}, u32[]{:S(2)}) collective-permute-start(f32[10,1,512]{2,1,0:T(1,128)S(1)} %get-tuple-element.87), channel_id=1, source_target_pairs={{8,0},{16,8},{24,16},{32,24},{40,32},{48,40},{56,48},{64,56},{72,6... | collective-permute-start | bytes 61448 | tf_op jit(solution)/shard_map/ppermute | solution.py:25
  262.5 5.9 %collective-permute-start.18 = (f32[10,64,1]{2,1,0:T(8,128)S(1)}, f32[10,64,1]{2,1,0:T(8,128)S(1)}, u32[]{:S(2)}, u32[]{:S(2)}) collective-permute-start(f32[10,64,1]{2,1,0:T(8,128)S(1)} %get-tuple-element.84), channel_id=1, source_target_pairs={{0,1},{1,2},{2,3},{3,4},{4,5},{5,6},{6,7},{8,9},{9,10},{10,11},{11... | collective-permute-start | bytes 7688 | tf_op jit(solution)/shard_map/ppermute | solution.py:24
  264.4 8.5 %copy-start.23 = (f32[10,64,513]{2,1,0:T(8,128)S(1)}, f32[10,64,513]{2,1,0:T(8,128)}, u32[]{:S(2)}) copy-start(f32[10,64,513]{2,1,0:T(8,128)} %get-tuple-element.71) | copy-start | bytes 3939844
  264.4 8.5 %collective-permute-start.19 = (f32[10,64,1]{2,1,0:T(8,128)S(1)}, f32[10,64,1]{2,1,0:T(8,128)S(1)}, u32[]{:S(2)}, u32[]{:S(2)}) collective-permute-start(f32[10,64,1]{2,1,0:T(8,128)S(1)} %get-tuple-element.85), channel_id=1, source_target_pairs={{1,0},{2,1},{3,2},{4,3},{5,4},{6,5},{7,6},{9,8},{10,9},{11,10},{12... | collective-permute-start | bytes 7688 | tf_op jit(solution)/shard_map/ppermute | solution.py:25
  268.2 6.0 %copy-start.10 = (f32[10,64,512]{2,1,0:T(8,128)S(1)}, f32[10,64,512]{2,1,0:T(8,128)}, u32[]{:S(2)}) copy-start(f32[10,64,512]{2,1,0:T(8,128)} %param.9) | copy-start | bytes 3932164
  268.2 6.0 %copy-start.32 = (f32[10,64,512]{2,1,0:T(8,128)S(1)}, f32[10,64,512]{2,1,0:T(8,128)}, u32[]{:S(2)}) copy-start(f32[10,64,512]{2,1,0:T(8,128)} %param.7) | copy-start | bytes 3932164
  268.2 6.0 %copy-start.43 = (f32[64,512]{1,0:T(8,128)S(1)}, f32[64,512]{1,0:T(8,128)}, u32[]{:S(2)}) copy-start(f32[64,512]{1,0:T(8,128)} %param.10) | copy-start | bytes 393220
  268.4 5.8 %copy-start.38 = (f32[10,64,1]{2,1,0:T(8,128)}, f32[10,64,1]{2,1,0:T(8,128)S(1)}, u32[]{:S(2)}) copy-start(f32[10,64,1]{2,1,0:T(8,128)S(1)} %collective-permute-done.18) | copy-start | bytes 7684
  318.2 9.8 %collective-permute-start.20 = (f32[10,1,512]{2,1,0:T(1,128)S(1)}, f32[10,1,512]{2,1,0:T(1,128)S(1)}, u32[]{:S(2)}, u32[]{:S(2)}) collective-permute-start(f32[10,1,512]{2,1,0:T(1,128)S(1)} %get-tuple-element.82), channel_id=1, source_target_pairs={{0,8},{8,16},{16,24},{24,32},{32,40},{40,48},{48,56},{56,64},{64,7... | collective-permute-start | bytes 61448 | tf_op jit(solution)/shard_map/ppermute | solution.py:24
  321.8 6.2 %collective-permute-start.21 = (f32[10,1,512]{2,1,0:T(1,128)S(1)}, f32[10,1,512]{2,1,0:T(1,128)S(1)}, u32[]{:S(2)}, u32[]{:S(2)}) collective-permute-start(f32[10,1,512]{2,1,0:T(1,128)S(1)} %get-tuple-element.83), channel_id=1, source_target_pairs={{8,0},{16,8},{24,16},{32,24},{40,32},{48,40},{56,48},{64,56},{72,6... | collective-permute-start | bytes 61448 | tf_op jit(solution)/shard_map/ppermute | solution.py:25
  323.3 6.6 %collective-permute-start.22 = (f32[10,64,1]{2,1,0:T(8,128)S(1)}, f32[10,64,1]{2,1,0:T(8,128)S(1)}, u32[]{:S(2)}, u32[]{:S(2)}) collective-permute-start(f32[10,64,1]{2,1,0:T(8,128)S(1)} %get-tuple-element.80), channel_id=1, source_target_pairs={{0,1},{1,2},{2,3},{3,4},{4,5},{5,6},{6,7},{8,9},{9,10},{10,11},{11... | collective-permute-start | bytes 7688 | tf_op jit(solution)/shard_map/ppermute | solution.py:24
  325.9 8.6 %copy-start.24 = (f32[10,64,513]{2,1,0:T(8,128)S(1)}, f32[10,64,513]{2,1,0:T(8,128)}, u32[]{:S(2)}) copy-start(f32[10,64,513]{2,1,0:T(8,128)} %get-tuple-element.71) | copy-start | bytes 3939844
  325.9 8.6 %copy-start.39 = (f32[10,64,1]{2,1,0:T(8,128)S(1)}, f32[10,64,1]{2,1,0:T(8,128)}, u32[]{:S(2)}) copy-start(f32[10,64,1]{2,1,0:T(8,128)} %copy-done.38) | copy-start | bytes 7684
  325.9 8.5 %copy-start.41 = (f32[10,64,1]{2,1,0:T(8,128)S(1)}, f32[10,64,1]{2,1,0:T(8,128)}, u32[]{:S(2)}) copy-start(f32[10,64,1]{2,1,0:T(8,128)} %copy-done.40) | copy-start | bytes 7684
  325.9 8.5 %collective-permute-start.23 = (f32[10,64,1]{2,1,0:T(8,128)S(1)}, f32[10,64,1]{2,1,0:T(8,128)S(1)}, u32[]{:S(2)}, u32[]{:S(2)}) collective-permute-start(f32[10,64,1]{2,1,0:T(8,128)S(1)} %get-tuple-element.81), channel_id=1, source_target_pairs={{1,0},{2,1},{3,2},{4,3},{5,4},{6,5},{7,6},{9,8},{10,9},{11,10},{12... | collective-permute-start | bytes 7688 | tf_op jit(solution)/shard_map/ppermute | solution.py:25
  329.8 7.9 %copy-start.11 = (f32[10,64,512]{2,1,0:T(8,128)S(1)}, f32[10,64,512]{2,1,0:T(8,128)}, u32[]{:S(2)}) copy-start(f32[10,64,512]{2,1,0:T(8,128)} %param.9) | copy-start | bytes 3932164
  329.8 7.9 %copy-start.15 = (f32[10,64,512]{2,1,0:T(8,128)S(1)}, f32[10,64,512]{2,1,0:T(8,128)}, u32[]{:S(2)}) copy-start(f32[10,64,512]{2,1,0:T(8,128)} %get-tuple-element.58) | copy-start | bytes 3932164
  388.3 2.7 copy-start.21
  391.0 6.9 %copy-start.3 = (f32[10,64,512]{2,1,0:T(8,128)}, f32[10,64,512]{2,1,0:T(8,128)S(1)}, u32[]{:S(2)}) copy-start(f32[10,64,512]{2,1,0:T(8,128)S(1)} %subtract_divide_fusion) | copy-start | bytes 3932164
  392.9 10.5 %collective-permute-start.24 = (f32[10,1,512]{2,1,0:T(1,128)S(1)}, f32[10,1,512]{2,1,0:T(1,128)S(1)}, u32[]{:S(2)}, u32[]{:S(2)}) collective-permute-start(f32[10,1,512]{2,1,0:T(1,128)S(1)} %get-tuple-element.78), channel_id=1, source_target_pairs={{0,8},{8,16},{16,24},{24,32},{32,40},{40,48},{48,56},{56,64},{64,7... | collective-permute-start | bytes 61448 | tf_op jit(solution)/shard_map/ppermute | solution.py:24
  396.5 6.9 %collective-permute-start.25 = (f32[10,1,512]{2,1,0:T(1,128)S(1)}, f32[10,1,512]{2,1,0:T(1,128)S(1)}, u32[]{:S(2)}, u32[]{:S(2)}) collective-permute-start(f32[10,1,512]{2,1,0:T(1,128)S(1)} %get-tuple-element.79), channel_id=1, source_target_pairs={{8,0},{16,8},{24,16},{32,24},{40,32},{48,40},{56,48},{64,56},{72,6... | collective-permute-start | bytes 61448 | tf_op jit(solution)/shard_map/ppermute | solution.py:25
  398.8 7.8 %collective-permute-start.26 = (f32[10,64,1]{2,1,0:T(8,128)}, f32[10,64,1]{2,1,0:T(8,128)S(1)}, u32[]{:S(2)}, u32[]{:S(2)}) collective-permute-start(f32[10,64,1]{2,1,0:T(8,128)} %get-tuple-element.76), channel_id=1, source_target_pairs={{0,1},{1,2},{2,3},{3,4},{4,5},{5,6},{6,7},{8,9},{9,10},{10,11},{11... | collective-permute-start | bytes 7688 | tf_op jit(solution)/shard_map/ppermute | solution.py:24
  400.7 8.9 %copy-start.4 = (f32[10,64,512]{2,1,0:T(8,128)S(1)}, f32[10,64,512]{2,1,0:T(8,128)}, u32[]{:S(2)}) copy-start(f32[10,64,512]{2,1,0:T(8,128)} %copy-done.3) | copy-start | bytes 3932164
  400.7 8.9 %copy-start.27 = (f32[10,64,513]{2,1,0:T(8,128)S(1)}, f32[10,64,513]{2,1,0:T(8,128)}, u32[]{:S(2)}) copy-start(f32[10,64,513]{2,1,0:T(8,128)} %get-tuple-element.55) | copy-start | bytes 3939844
  400.7 8.9 %copy-start.28 = (f32[10,64,513]{2,1,0:T(8,128)S(1)}, f32[10,64,513]{2,1,0:T(8,128)}, u32[]{:S(2)}) copy-start(f32[10,64,513]{2,1,0:T(8,128)} %get-tuple-element.56) | copy-start | bytes 3939844
  400.7 8.9 %collective-permute-start.27 = (f32[10,64,1]{2,1,0:T(8,128)}, f32[10,64,1]{2,1,0:T(8,128)S(1)}, u32[]{:S(2)}, u32[]{:S(2)}) collective-permute-start(f32[10,64,1]{2,1,0:T(8,128)} %get-tuple-element.77), channel_id=1, source_target_pairs={{1,0},{2,1},{3,2},{4,3},{5,4},{6,5},{7,6},{9,8},{10,9},{11,10},{12... | collective-permute-start | bytes 7688 | tf_op jit(solution)/shard_map/ppermute | solution.py:25
  411.7 63.0 %copy-start.5 = (f32[10,64,512]{2,1,0:T(8,128)S(1)}, f32[10,64,512]{2,1,0:T(8,128)}, u32[]{:S(2)}) copy-start(f32[10,64,512]{2,1,0:T(8,128)} %copy-done.3) | copy-start | bytes 3932164
  (13 other events, 21.9 us)
